TPU v7x, 128 devices: a whole 4x4x4 slice. The times are simulated.
128 devices in a mesh: fsdp: 32 (over z, y, x_hi), sp: 4 (over x_lo, core).
Axes of the slice: x: 4 (x_hi: 2, x_lo: 2; x = x_hi * 2 + x_lo), y: 4, z: 4, core: 2. Of those that a mesh axis runs over, the one named last changes fastest.
Arguments:
- tokens: bfloat16 [32, 512, 1536], P('fsdp', 'sp'), may hold values from -6 to 6
- modulation: float32 [32, 1, 6, 1536], P('fsdp'), may hold values from -4 to 4
- w_qkv: bfloat16 [1, 1536, 3, 1536], P(None, 'fsdp', None, 'sp'), may hold values from -0.15625 to 0.15625
- w_out: bfloat16 [1, 1536, 1536], P(None, 'sp', 'fsdp'), may hold values from -0.15625 to 0.15625
- w_in: bfloat16 [1, 1536, 6144], P(None, 'fsdp', 'sp'), may hold values from -0.15625 to 0.15625
- w_back: bfloat16 [1, 6144, 1536], P(None, 'sp', 'fsdp'), may hold values from -0.078125 to 0.078125
- out_grad: bfloat16 [32, 512, 1536], P('fsdp', 'sp'), may hold values from -6 to 6
Outputs:
- final_out: bfloat16 [32, 512, 1536], P('fsdp', 'sp')
- input_grad: float32 [32, 512, 1536], P('fsdp', 'sp')
- grad_qkv: float32 [1, 1536, 3, 1536], P(None, 'fsdp', None, 'sp')
- grad_out: float32 [1, 1536, 1536], P(None, 'sp', 'fsdp')
- grad_in: float32 [1, 1536, 6144], P(None, 'fsdp', 'sp')
- grad_back: float32 [1, 6144, 1536], P(None, 'sp', 'fsdp')
All inputs are finite; a program needn't handle non-finite values.
Results may differ from a plain program's by a relative error of at most 0.03.
Values may be sent and summed in bfloat16 or wider, within the bound.
A program may use at most 128 MiB of HBM per device.

v0:
```python
import functools
import math

import jax
import jax.numpy as jnp
from jax import lax
from jax.experimental import pallas as pl
from jax.experimental.pallas import tpu as pltpu
from jax.sharding import PartitionSpec as P

HEAD_DIM = 128
LN_EPS = 1e-06
TEMPER = 2.5
F32 = jnp.float32
BF16 = jnp.bfloat16
MESH = pl.DeviceIdType.MESH
GROUP = 1536
HALF = GROUP // 2
QUART = GROUP // 4
ROWS = 48


def rem(a, n):
    return lax.rem(a, n)


class Place:
    def __init__(self):
        f = lax.axis_index("fsdp")
        s = lax.axis_index("sp")
        self.z, self.y, self.xh = lax.div(f, 8), rem(lax.div(f, 2), 4), rem(f, 2)
        self.xl, self.c = lax.div(s, 2), rem(s, 2)
        self.s = s

    def dev(self, **kw):
        v = {k: kw.get(k, getattr(self, k)) for k in ("z", "y", "xh", "xl", "c")}
        return (v["z"] * 8 + v["y"] * 2 + v["xh"], v["xl"] * 2 + v["c"])

    def ring(self, axis, step):
        return rem(getattr(self, axis) + step + 4, 4)

    def near(self, axis, step):
        return self.dev(**{axis: self.ring(axis, step)})

    def across(self):
        return self.dev(xh=1 - self.xh)

    def chip(self):
        return self.dev(xl=1 - self.xl)

    def core(self):
        return self.dev(c=1 - self.c)


def greet(devices):
    barrier = pltpu.get_barrier_semaphore()
    for d in devices:
        pl.semaphore_signal(barrier, inc=1, device_id=d, device_id_type=MESH)
    pl.semaphore_wait(barrier, len(devices))


def torus_peers(me):
    return [me.near(a, s) for a in ("z", "y") for s in (1, -1)] + [me.across()]


class Sends:
    def __init__(self):
        self.open = []

    def start(self, src, dst, ssem, rsem, dev):
        copy = pltpu.make_async_remote_copy(
            src_ref=src, dst_ref=dst, send_sem=ssem, recv_sem=rsem, device_id=dev, device_id_type=MESH
        )
        copy.start()
        self.open.append(copy)

    def close(self):
        for copy in self.open:
            copy.wait_send()
        self.open = []


def arrive(ref, rsem, dev):
    pltpu.make_async_remote_copy(
        src_ref=ref, dst_ref=ref, send_sem=rsem, recv_sem=rsem, device_id=dev, device_id_type=MESH
    ).wait_recv()


class Gather:
    def __init__(self, me, w, half, col, xb, ssem, rsem, sends):
        self.me, self.w, self.xb, self.ssem, self.rsem, self.sends = me, w, xb, ssem, rsem, sends
        self.axes = ("y", "z") if half == 0 else ("z", "y")
        self.c0 = col + half * HALF

    def part(self, level, step, cols):
        axis = self.axes[level]
        at = {"z": self.me.z, "y": self.me.y}
        at[axis] = self.me.ring(axis, step)
        if level == 1:
            at[self.axes[0]] = slice(None)
        return self.w.at[at["z"], at["y"], self.xb, :, cols]

    def cols(self, which):
        return {
            "all": pl.ds(self.c0, HALF),
            "lo": pl.ds(self.c0, QUART),
            "hi": pl.ds(self.c0 + QUART, QUART),
        }[which]

    def go(self, level, step, which, to, i):
        ref = self.part(level, step, self.cols(which))
        i = level * 4 + i
        self.sends.start(ref, ref, self.ssem.at[i], self.rsem.at[i], self.me.near(self.axes[level], to))

    def got(self, level, step, which, i):
        arrive(self.part(level, step, self.cols(which)), self.rsem.at[level * 4 + i], self.me.near(self.axes[level], 1))

    def first(self, level):
        self.go(level, 0, "all", 1, 0)
        self.go(level, 0, "all", -1, 1)

    def second(self, level):
        self.got(level, -1, "all", 0)
        self.go(level, -1, "lo", 1, 2)
        self.got(level, 1, "all", 1)
        self.go(level, 1, "hi", -1, 3)

    def last(self, level):
        self.got(level, 2, "lo", 2)
        self.got(level, 2, "hi", 3)


def wider(ref_value):
    return ref_value.astype(F32)


class Scatter:
    def __init__(self, me, g, half, col, xb, bufs, ssem, rsem, sends):
        self.me, self.g, self.xb, self.ssem, self.rsem, self.sends = me, g, xb, ssem, rsem, sends
        self.axes = ("z", "y") if half == 0 else ("y", "z")
        self.c0 = col + half * HALF
        self.bufs = bufs

    def spot(self, level, step, which):
        axis = self.axes[level]
        at = {"z": self.me.z, "y": self.me.y}
        at[axis] = self.me.ring(axis, step)
        if level == 0:
            at[self.axes[1]] = slice(None)
        cols = {
            "all": pl.ds(self.c0, HALF),
            "lo": pl.ds(self.c0, QUART),
            "hi": pl.ds(self.c0 + QUART, QUART),
        }[which]
        return (at["z"], at["y"], self.xb, slice(None), cols)

    def far(self, level):
        for to, which, i in ((1, "lo", 0), (-1, "hi", 1)):
            j = level * 4 + i
            self.sends.start(
                self.g.at[self.spot(level, 2, which)], self.bufs[level][0].at[i],
                self.ssem.at[j], self.rsem.at[j], self.me.near(self.axes[level], to),
            )

    def relay(self, level):
        for to, which, i in ((1, "lo", 0), (-1, "hi", 1)):
            buf = self.bufs[level][0].at[i]
            arrive(buf, self.rsem.at[level * 4 + i], self.me.near(self.axes[level], -to))
            spot = self.spot(level, to, which)
            self.g[spot] = (wider(self.g[spot]) + wider(buf[...])).astype(BF16)
        for to, i in ((1, 0), (-1, 1)):
            j = level * 4 + 2 + i
            self.sends.start(
                self.g.at[self.spot(level, to, "all")], self.bufs[level][1].at[i],
                self.ssem.at[j], self.rsem.at[j], self.me.near(self.axes[level], to),
            )

    def total(self, level):
        near = self.bufs[level][1]
        for to, i in ((1, 0), (-1, 1)):
            arrive(near.at[i], self.rsem.at[level * 4 + 2 + i], self.me.near(self.axes[level], -to))
        spot = self.spot(level, 0, "all")
        return spot, wider(self.g[spot]) + wider(near[0]) + wider(near[1])

    def fold(self):
        spot, total = self.total(0)
        self.g[spot] = total.astype(BF16)


def gather_kernel(b_ref, w_ref, ssem, rsem, xs, xr, csem):
    me = Place()
    own = pltpu.make_async_copy(b_ref, w_ref.at[me.z, me.y, me.xh], csem)
    own.start()
    greet(torus_peers(me))
    own.wait()
    sends = Sends()
    pieces = []
    for group in range(3):
        for side in range(2):
            xb = me.xh if side == 0 else 1 - me.xh
            k = (group * 2 + side) * 2
            pieces.append(
                [Gather(me, w_ref, h, group * GROUP, xb, ssem.at[k + h], rsem.at[k + h], sends) for h in range(2)]
            )

    def each(k, what, *args):
        if 0 <= k < len(pieces):
            if what == "first" and args[0] == 0 and k % 2 == 1:
                cols = pl.ds(k // 2 * GROUP, GROUP)
                arrive(w_ref.at[me.z, me.y, 1 - me.xh, :, cols], xr.at[k // 2], me.across())
            for half in pieces[k]:
                getattr(half, what)(*args)

    for group in range(3):
        ref = w_ref.at[me.z, me.y, me.xh, :, pl.ds(group * GROUP, GROUP)]
        sends.start(ref, ref, xs.at[group], xr.at[group], me.across())
    each(0, "first", 0)
    each(0, "second", 0)
    each(1, "first", 0)
    each(0, "last", 0)
    for k in range(len(pieces) + 1):
        each(k, "first", 1)
        each(k + 2, "first", 0)
        each(k + 1, "second", 0)
        each(k - 1, "last", 1)
        each(k, "second", 1)
        each(k + 1, "last", 0)
    sends.close()


def scatter_kernel(g_ref, o_ref, r1, r2, p1, p2, xbuf, part, ssem, rsem, xs, xr):
    me = Place()
    greet(torus_peers(me))
    sends = Sends()
    pieces = []
    for n, group in enumerate((2, 1, 0)):
        for side in range(2):
            xb = 1 - me.xh if side == 0 else me.xh
            k = n * 2 + side
            halves = []
            for h in range(2):
                bufs = ((r1.at[k % 3, h], r2.at[k % 3, h]), (p1.at[k % 3, h], p2.at[k % 3, h]))
                halves.append(
                    Scatter(me, g_ref, h, group * GROUP, xb, bufs, ssem.at[k * 2 + h], rsem.at[k * 2 + h], sends)
                )
            pieces.append((group, side, halves))

    def each(k, what, *args):
        if 0 <= k < len(pieces):
            for half in pieces[k][2]:
                getattr(half, what)(*args)

    def finish(k):
        if not 0 <= k < len(pieces):
            return
        group, side, halves = pieces[k]
        for h, half in enumerate(halves):
            spot, total = half.total(1)
            cols = pl.ds(group * GROUP + h * HALF, HALF)
            if side == 0:
                part[:, cols] = total.astype(BF16)
            else:
                o_ref[:, cols] = total
        if side == 0:
            cols = pl.ds(group * GROUP, GROUP)
            sends.start(part.at[:, cols], xbuf.at[:, cols], xs.at[group], xr.at[group], me.across())
        else:
            cols = pl.ds(group * GROUP, GROUP)
            arrive(xbuf.at[:, cols], xr.at[group], me.across())
            o_ref[:, cols] += wider(xbuf[:, cols])

    each(0, "far", 0)
    for t in range(len(pieces) + 3):
        each(t + 1, "far", 0)
        each(t, "relay", 0)
        each(t - 1, "fold")
        each(t - 1, "far", 1)
        each(t - 2, "relay", 1)
        finish(t - 3)
    sends.close()


DMA = pltpu.SemaphoreType.DMA
VM = pl.BlockSpec(memory_space=pltpu.VMEM)


def params(cid):
    return pltpu.CompilerParams(collective_id=cid, has_side_effects=True, vmem_limit_bytes=60 * 2**20)


def torus_gather(block):
    return pl.pallas_call(
        gather_kernel,
        out_shape=jax.ShapeDtypeStruct((4, 4, 2, ROWS, 3 * GROUP), BF16),
        in_specs=[VM],
        out_specs=VM,
        scratch_shapes=[DMA((12, 8)), DMA((12, 8)), DMA((3,)), DMA((3,)), DMA],
        compiler_params=params(0),
        cost_estimate=pl.CostEstimate(flops=10**10, bytes_accessed=3 * 10**7, transcendentals=0),
    )(block)


def torus_scatter(grads):
    return pl.pallas_call(
        scatter_kernel,
        out_shape=jax.ShapeDtypeStruct((ROWS, 3 * GROUP), F32),
        in_specs=[VM],
        out_specs=VM,
        scratch_shapes=[
            pltpu.VMEM((3, 2, 2, 4, ROWS, QUART), BF16),
            pltpu.VMEM((3, 2, 2, 4, ROWS, HALF), BF16),
            pltpu.VMEM((3, 2, 2, ROWS, QUART), BF16),
            pltpu.VMEM((3, 2, 2, ROWS, HALF), BF16),
            pltpu.VMEM((ROWS, 3 * GROUP), BF16),
            pltpu.VMEM((ROWS, 3 * GROUP), BF16),
            DMA((12, 8)), DMA((12, 8)), DMA((3,)), DMA((3,)),
        ],
        compiler_params=params(1),
        cost_estimate=pl.CostEstimate(flops=10**10, bytes_accessed=3 * 10**7, transcendentals=0),
    )(grads)


def seq_gather_kernel(b_ref, o_ref, ss, rs, csem):
    me = Place()
    own = pltpu.make_async_copy(b_ref, o_ref.at[me.s], csem)
    own.start()
    greet([me.chip(), me.core()])
    own.wait()
    sends = Sends()
    sends.start(o_ref.at[me.s], o_ref.at[me.s], ss.at[0], rs.at[0], me.chip())
    sends.start(o_ref.at[me.s], o_ref.at[me.s], ss.at[1], rs.at[1], me.core())
    other = (1 - me.xl) * 2 + me.c
    arrive(o_ref.at[other], rs.at[0], me.chip())
    sends.start(o_ref.at[other], o_ref.at[other], ss.at[2], rs.at[2], me.core())
    arrive(o_ref.at[me.xl * 2 + 1 - me.c], rs.at[1], me.core())
    arrive(o_ref.at[(1 - me.xl) * 2 + 1 - me.c], rs.at[2], me.core())
    sends.close()


def seq_gather(block, cid):
    own, width = block.shape
    return pl.pallas_call(
        seq_gather_kernel,
        out_shape=jax.ShapeDtypeStruct((4, own, width), BF16),
        in_specs=[VM],
        out_specs=VM,
        scratch_shapes=[DMA((3,)), DMA((3,)), DMA],
        compiler_params=params(cid),
    )(block).reshape(4 * own, width)


def seq_scatter_kernel(p_ref, o_ref, swap, mine, theirs, ss, rs):
    me = Place()
    greet([me.chip(), me.core()])
    sends = Sends()
    for i, xl in enumerate((1 - me.xl, me.xl)):
        sends.start(p_ref.at[xl * 2 + 1 - me.c], swap.at[i], ss.at[i], rs.at[i], me.core())
    arrive(swap.at[0], rs.at[0], me.core())
    mine[...] = (wider(p_ref[(1 - me.xl) * 2 + me.c]) + wider(swap[0])).astype(BF16)
    sends.start(mine, theirs, ss.at[2], rs.at[2], me.chip())
    arrive(swap.at[1], rs.at[1], me.core())
    o_ref[...] = wider(p_ref[me.s]) + wider(swap[1])
    arrive(theirs, rs.at[2], me.chip())
    o_ref[...] += wider(theirs[...])
    sends.close()


def seq_scatter(whole, cid):
    rows, width = whole.shape
    own = rows // 4
    return pl.pallas_call(
        seq_scatter_kernel,
        out_shape=jax.ShapeDtypeStruct((own, width), F32),
        in_specs=[VM],
        out_specs=VM,
        scratch_shapes=[
            pltpu.VMEM((2, own, width), BF16), pltpu.VMEM((own, width), BF16), pltpu.VMEM((own, width), BF16),
            DMA((3,)), DMA((3,)),
        ],
        compiler_params=params(cid),
    )(whole.reshape(4, own, width))


def normalize(stream):
    centred = stream - jnp.mean(stream, axis=-1, keepdims=True)
    rstd = lax.rsqrt(jnp.mean(centred * centred, axis=-1, keepdims=True) + LN_EPS)
    return (centred * rstd, rstd)


def norm_back(normed, rstd, incoming):
    first = jnp.mean(incoming, axis=-1, keepdims=True)
    second = jnp.mean(incoming * normed, axis=-1, keepdims=True)
    return rstd * (incoming - first - normed * second)


def gelu_tanh(hidden):
    return jax.nn.gelu(hidden, approximate=True)


def contract(left, right, left_dim, right_dim):
    return lax.dot_general(
        left, right, (((left_dim,), (right_dim,)), ((), ())), preferred_element_type=F32
    )


def softmax_rows(queries, key_rows, factor):
    scores = contract(queries, key_rows, 1, 1) * factor
    scores = jnp.exp(scores - jnp.max(scores, axis=-1, keepdims=True))
    return scores * (1.0 / jnp.sum(scores, axis=-1, keepdims=True))


def attend_kernel(factor, q_ref, k_ref, v_ref, o_ref):
    probs = softmax_rows(q_ref[...], k_ref[...], factor)
    o_ref[...] = contract(probs.astype(BF16), v_ref[...], 1, 0).astype(BF16)


def attend_back_kernel(factor, heads, q_ref, k_ref, v_ref, do_ref, out_ref):
    head = pl.program_id(0)
    queries, key_rows, upstream = q_ref[...], k_ref[...], do_ref[...]
    probs = softmax_rows(queries, key_rows, factor)
    dprobs = contract(upstream, v_ref[...], 1, 1)
    dscores = probs * (dprobs - jnp.sum(probs * dprobs, axis=-1, keepdims=True)) * factor
    dscores = dscores.astype(BF16)
    parts = (
        contract(dscores, key_rows, 1, 0),
        contract(dscores, queries, 0, 0),
        contract(probs.astype(BF16), upstream, 0, 0),
    )
    for place, part in enumerate(parts):
        column = pl.multiple_of((place * heads + head) * HEAD_DIM, HEAD_DIM)
        out_ref[:, pl.ds(column, HEAD_DIM)] = part.astype(BF16)


def column_spec(seq, heads, place):
    return pl.BlockSpec((seq, HEAD_DIM), lambda head: (0, place * heads + head))


def attend(packed, heads, factor):
    seq = packed.shape[0]
    return pl.pallas_call(
        functools.partial(attend_kernel, factor),
        out_shape=jax.ShapeDtypeStruct((seq, heads * HEAD_DIM), BF16),
        grid=(heads,),
        in_specs=[column_spec(seq, heads, place) for place in range(3)],
        out_specs=column_spec(seq, heads, 0),
    )(packed, packed, packed)


def attend_back(packed, upstream, heads, factor):
    seq = packed.shape[0]
    return pl.pallas_call(
        functools.partial(attend_back_kernel, factor, heads),
        out_shape=jax.ShapeDtypeStruct(packed.shape, BF16),
        grid=(heads,),
        in_specs=[column_spec(seq, heads, place) for place in (0, 1, 2, 0)],
        out_specs=pl.BlockSpec((seq, packed.shape[1]), lambda head: (0, 0)),
    )(packed, packed, packed, upstream)


def local(tokens, modulation, w_qkv, w_out, w_in, w_back, out_grad):
    _, own, width = tokens.shape
    own_width = w_qkv.shape[3]
    heads = own_width // HEAD_DIM
    factor = TEMPER / math.sqrt(HEAD_DIM)
    grad_scale = 1.0 / math.sqrt(own * lax.axis_size("sp") * lax.axis_size("fsdp"))

    def grad_term(left, right):
        return (contract(left, right, 0, 0) * grad_scale).astype(BF16)

    stream = tokens[0].astype(F32)
    mod = modulation[0, 0][:, None, :]
    block = jnp.concatenate([w_qkv[0].reshape(ROWS, 3 * own_width), w_out[0].T, w_in[0], w_back[0].T], axis=1)
    whole = torus_gather(block).reshape(width, 3 * GROUP)
    joint, whole_out = whole[:, : 3 * own_width], whole[:, 3 * own_width : GROUP]
    whole_in, whole_back = whole[:, GROUP : 2 * GROUP], whole[:, 2 * GROUP :]

    n1, r1 = normalize(stream)
    a1 = seq_gather((n1 * (1.0 + mod[1]) + mod[0]).astype(BF16), 2)
    packed = contract(a1, joint, 1, 0).astype(BF16)
    attended = attend(packed, heads, factor)
    middle = stream + mod[2] * seq_scatter(contract(attended, whole_out, 1, 1).astype(BF16), 3)
    n2, r2 = normalize(middle)
    a2 = seq_gather((n2 * (1.0 + mod[4]) + mod[3]).astype(BF16), 4)
    hidden = contract(a2, whole_in, 1, 0)
    active = gelu_tanh(hidden).astype(BF16)
    final = middle + mod[5] * seq_scatter(contract(active, whole_back, 1, 1).astype(BF16), 5)
    grad = out_grad[0].astype(F32)
    dm = seq_gather((mod[5] * grad).astype(BF16), 6)
    dg = contract(dm, whole_back, 1, 0)
    _, pullback = jax.vjp(gelu_tanh, hidden)
    du = pullback(dg)[0].astype(BF16)
    back_second = seq_scatter(contract(du, whole_in, 1, 1).astype(BF16), 7)
    grad = grad + norm_back(n2, r2, back_second * (1.0 + mod[4]))
    da = seq_gather((mod[2] * grad).astype(BF16), 8)
    do = contract(da, whole_out, 1, 0).astype(BF16)
    dqkv = attend_back(packed, do, heads, factor)
    back_first = seq_scatter(contract(dqkv, joint, 1, 1).astype(BF16), 9)
    grad = grad + norm_back(n1, r1, back_first * (1.0 + mod[1]))
    terms = jnp.concatenate(
        [grad_term(a1, dqkv), grad_term(da, attended), grad_term(a2, du), grad_term(dm, active)], axis=1
    )
    sums = torus_scatter(terms.reshape(4, 4, 2, ROWS, 3 * GROUP))
    return (
        final.astype(BF16)[None],
        grad[None],
        sums[:, : 3 * own_width].reshape(1, ROWS, 3, own_width),
        sums[:, 3 * own_width : GROUP].T[None],
        sums[:, GROUP : 2 * GROUP][None],
        sums[:, 2 * GROUP :].T[None],
    )


def solution(mesh):
    weights = (
        P(None, "fsdp", None, "sp"),
        P(None, "sp", "fsdp"),
        P(None, "fsdp", "sp"),
        P(None, "sp", "fsdp"),
    )
    rows = P("fsdp", "sp", None)
    return jax.shard_map(
        local,
        mesh=mesh,
        in_specs=(rows, P("fsdp", None, None, None), *weights, rows),
        out_specs=(rows, rows, *weights),
        check_vma=False,
    )
```

profile of v0, /device:TPU:1, one launch (start us, length us, event | category | flops | bytes accessed | tf_op | source)
XLA Modules:
  0.0 443.0 jit_solution(15672651559428447305)
XLA Ops:
  6.3 16.4 %shard_map.118 = bf16[4,128,1536]{2,1,0:T(8,128)(2,1)} custom-call(bf16[128,1536]{1,0:T(8,128)(2,1)} %get-tuple-element.35.b_ref), custom_call_target="tpu_custom_call" | custom-call | tf_op jit(solution)/shard_map/pallas_call | solution.py:342
  23.7 89.6 %shard_map.119 = bf16[4,4,2,48,4608]{4,3,2,1,0:T(8,128)(2,1)} custom-call(bf16[48,4608]{1,0:T(8,128)(2,1)} %pad_maximum_fusion.1.b_ref), custom_call_target="tpu_custom_call" | custom-call | flops 10000000000 | bytes 30000000 | tf_op jit(solution)/shard_map/pallas_call | solution.py:292
  113.3 5.3 %fusion.24.q_ref.k_ref.v_ref = bf16[512,1152]{1,0:T(8,128)(2,1)} fusion(bf16[512,1536]{1,0:T(8,128)(2,1)S(1)} %bitcast.91, bf16[1536,4608]{1,0:T(8,128)(2,1)} %bitcast.104), kind=kOutput, calls=%fused_computation.30 | convolution fusion | flops 1812529152 | bytes 6291456 | tf_op jit(solution)/shard_map/dot_general | solution.py:401
  118.6 4.7 %shard_map.120 = bf16[512,384]{1,0:T(8,128)(2,1)} custom-call(bf16[512,1152]{1,0:T(8,128)(2,1)} %fusion.24.q_ref.k_ref.v_ref, bf16[512,1152]{1,0:T(8,128)(2,1)} %fusion.24.q_ref.k_ref.v_ref, bf16[512,1152]{1,0:T(8,128)(2,1)} %fusion.24.q_ref.k_ref.v_ref), custom_call_target="tpu_custom_call" | custom-call | tf_op jit(solution)/shard_map/pallas_call | solution.py:440
  123.3 3.6 convolution_convert_fusion
  126.9 18.9 %shard_map.121 = f32[128,1536]{1,0:T(8,128)} custom-call(bf16[4,128,1536]{2,1,0:T(8,128)(2,1)} %bitcast.88), custom_call_target="tpu_custom_call" | custom-call | tf_op jit(solution)/shard_map/pallas_call | solution.py:371
  148.3 15.1 %shard_map.122 = bf16[4,128,1536]{2,1,0:T(8,128)(2,1)} custom-call(bf16[128,1536]{1,0:T(8,128)(2,1)} %add_convert_fusion.1.b_ref), custom_call_target="tpu_custom_call" | custom-call | tf_op jit(solution)/shard_map/pallas_call | solution.py:342
  163.5 7.1 %fusion.9 = f32[512,1536]{1,0:T(8,128)} fusion(bf16[512,1536]{1,0:T(8,128)(2,1)} %bitcast.93, bf16[1536,4608]{1,0:T(8,128)(2,1)} %bitcast.106), kind=kOutput, calls=%fused_computation.15 | convolution fusion | flops 2415919104 | bytes 9437184 | tf_op jit(solution)/shard_map/dot_general | solution.py:401
  170.5 15.2 %shard_map.124 = bf16[4,128,1536]{2,1,0:T(8,128)(2,1)} custom-call(bf16[128,1536]{1,0:T(8,128)(2,1)} %get-tuple-element.36.b_ref), custom_call_target="tpu_custom_call" | custom-call | tf_op jit(solution)/shard_map/pallas_call | solution.py:342
  185.7 7.8 %fusion.17 = bf16[512,1536]{1,0:T(8,128)(2,1)S(1)} fusion(f32[512,1536]{1,0:T(8,128)} %fusion.9, bf16[512,1536]{1,0:T(8,128)(2,1)} %bitcast.95, bf16[1536,4608]{1,0:T(8,128)(2,1)} %bitcast.107), kind=kOutput, calls=%fused_computation.23 | convolution fusion | flops 2431647744 | bytes 11010048 | tf_op jit(solution)/shard_map/dot_general | solution.py:401
  193.6 6.6 %fusion.30 = bf16[512,1536]{1,0:T(8,128)(2,1)} fusion(bf16[512,1536]{1,0:T(8,128)(2,1)S(1)} %fusion.17, bf16[1536,4608]{1,0:T(8,128)(2,1)} %bitcast.108), kind=kOutput, calls=%fused_computation.32 | convolution fusion | flops 2416705536 | bytes 7864320 | tf_op jit(solution)/shard_map/dot_general | solution.py:401
  200.2 15.0 %shard_map.125 = f32[128,1536]{1,0:T(8,128)} custom-call(bf16[4,128,1536]{2,1,0:T(8,128)(2,1)} %bitcast.89), custom_call_target="tpu_custom_call" | custom-call | tf_op jit(solution)/shard_map/pallas_call | solution.py:371
  216.7 7.3 %fusion.33 = bf16[512,1536]{1,0:T(8,128)(2,1)} fusion(bf16[1536,4608]{1,0:T(8,128)(2,1)} %bitcast.109, f32[512,1536]{1,0:T(8,128)} %fusion.9), kind=kOutput, calls=%fused_computation.33 | convolution fusion | flops 2423783424 | bytes 9437184 | tf_op jit(solution)/shard_map/dot_general | solution.py:401
  224.0 15.6 %shard_map.123 = f32[128,1536]{1,0:T(8,128)} custom-call(bf16[4,128,1536]{2,1,0:T(8,128)(2,1)} %bitcast.90), custom_call_target="tpu_custom_call" | custom-call | tf_op jit(solution)/shard_map/pallas_call | solution.py:371
  242.1 15.1 %shard_map.126 = bf16[4,128,1536]{2,1,0:T(8,128)(2,1)} custom-call(bf16[128,1536]{1,0:T(8,128)(2,1)} %get-tuple-element.28.b_ref), custom_call_target="tpu_custom_call" | custom-call | tf_op jit(solution)/shard_map/pallas_call | solution.py:342
  257.3 3.5 convolution_convert_fusion.1.do_ref
  260.7 6.5 %shard_map.127 = bf16[512,1152]{1,0:T(8,128)(2,1)} custom-call(bf16[512,1152]{1,0:T(8,128)(2,1)} %fusion.24.q_ref.k_ref.v_ref, bf16[512,1152]{1,0:T(8,128)(2,1)} %fusion.24.q_ref.k_ref.v_ref, bf16[512,1152]{1,0:T(8,128)(2,1)} %fusion.24.q_ref.k_ref.v_ref, bf16[512,384]{1,0:T(8,128)(2,1)} %convolution_convert_fusion.1.do_ref), custom_call_target="tpu_custom_call" | custom-call | tf_op jit(solution)/shard_map/pallas_call | solution.py:451
  267.2 5.8 %fusion.27 = bf16[512,1536]{1,0:T(8,128)(2,1)} fusion(bf16[512,1152]{1,0:T(8,128)(2,1)} %shard_map.127, bf16[1536,4608]{1,0:T(8,128)(2,1)} %bitcast.111), kind=kOutput, calls=%fused_computation.31 | convolution fusion | flops 1812725760 | bytes 6291456 | tf_op jit(solution)/shard_map/dot_general | solution.py:401
  273.0 15.1 %shard_map.128 = f32[128,1536]{1,0:T(8,128)} custom-call(bf16[4,128,1536]{2,1,0:T(8,128)(2,1)} %bitcast.87), custom_call_target="tpu_custom_call" | custom-call | tf_op jit(solution)/shard_map/pallas_call | solution.py:371
  292.1 3.2 fusion.1
  295.3 3.1 fusion
  302.2 32.6 %pad_maximum_fusion = bf16[1536,4608]{0,1:T(8,128)(2,1)} fusion(bf16[1536,1536]{0,1:T(8,128)(2,1)S(1)} %fusion.1, bf16[1536,1536]{0,1:T(8,128)(2,1)S(1)} %fusion, bf16[1536,384]{0,1:T(8,128)(2,1)S(1)} %fusion.36, bf16[1536,1152]{0,1:T(8,128)(2,1)S(1)} %fusion.2), kind=kLoop, calls=%fused_computation | loop fusion | flops 56623104 | bytes 28311552 | tf_op jit(solution)/shard_map/concatenate | solution.py:499
  334.9 18.8 %copy.17 = bf16[1536,4608]{1,0:T(8,128)(2,1)} copy(bf16[1536,4608]{0,1:T(8,128)(2,1)} %pad_maximum_fusion) | data formatting | bytes 28311552 | tf_op jit(solution)/shard_map/concatenate | solution.py:499
  353.6 84.1 %shard_map.129 = f32[48,4608]{1,0:T(8,128)} custom-call(bf16[4,4,2,48,4608]{4,3,2,1,0:T(8,128)(2,1)} %bitcast.86), custom_call_target="tpu_custom_call" | custom-call | flops 10000000000 | bytes 30000000 | tf_op jit(solution)/shard_map/pallas_call | solution.py:304
  (63 shorter events, 25.8 us)
Async XLA Ops:
  0.6 22.2 %copy-start.10 = (bf16[1,1536,48]{1,2,0:T(8,128)(2,1)S(1)}, bf16[1,1536,48]{1,2,0:T(8,128)(2,1)}, u32[]{:S(2)}) copy-start(bf16[1,1536,48]{1,2,0:T(8,128)(2,1)} %param.12) | copy-start | bytes 442372
  0.6 22.2 %copy-start.11 = (bf16[1,48,1536]{2,1,0:T(8,128)(2,1)S(1)}, bf16[1,48,1536]{2,1,0:T(8,128)(2,1)}, u32[]{:S(2)}) copy-start(bf16[1,48,1536]{2,1,0:T(8,128)(2,1)} %param.11) | copy-start | bytes 442372
  0.7 22.2 %copy-start.13 = (bf16[1,384,48]{1,2,0:T(8,128)(2,1)S(1)}, bf16[1,384,48]{1,2,0:T(8,128)(2,1)}, u32[]{:S(2)}) copy-start(bf16[1,384,48]{1,2,0:T(8,128)(2,1)} %param.10) | copy-start | bytes 110596
  0.7 22.1 %copy-start.12 = (bf16[1,48,3,384]{3,1,2,0:T(8,128)(2,1)S(1)}, bf16[1,48,3,384]{3,1,2,0:T(8,128)(2,1)}, u32[]{:S(2)}) copy-start(bf16[1,48,3,384]{3,1,2,0:T(8,128)(2,1)} %param.9) | copy-start | bytes 331780
  23.7 89.6 %copy-start.2 = (bf16[4,128,1536]{2,1,0:T(8,128)(2,1)S(1)}, bf16[4,128,1536]{2,1,0:T(8,128)(2,1)}, u32[]{:S(2)}) copy-start(bf16[4,128,1536]{2,1,0:T(8,128)(2,1)} %shard_map.118) | copy-start | bytes 4718596
  123.3 22.5 %copy-start = (bf16[1,128,1536]{2,1,0:T(8,128)(2,1)S(1)}, bf16[1,128,1536]{2,1,0:T(8,128)(2,1)}, u32[]{:S(2)}) copy-start(bf16[1,128,1536]{2,1,0:T(8,128)(2,1)} %param.7) | copy-start | bytes 1179652
  193.6 6.7 %copy-start.15 = (bf16[512,1536]{1,0:T(8,128)(2,1)}, bf16[512,1536]{1,0:T(8,128)(2,1)S(1)}, u32[]{:S(2)}) copy-start(bf16[512,1536]{1,0:T(8,128)(2,1)S(1)} %fusion.17) | copy-start | bytes 4718596
  216.6 23.0 %copy-start.1 = (f32[128,1536]{1,0:T(8,128)S(1)}, f32[128,1536]{1,0:T(8,128)}, u32[]{:S(2)}) copy-start(f32[128,1536]{1,0:T(8,128)} %shard_map.125) | copy-start | bytes 2359300
  216.6 23.0 %copy-start.7 = (bf16[1,128,1536]{2,1,0:T(8,128)(2,1)S(1)}, bf16[1,128,1536]{2,1,0:T(8,128)(2,1)}, u32[]{:S(2)}) copy-start(bf16[1,128,1536]{2,1,0:T(8,128)(2,1)} %param.13) | copy-start | bytes 1179652
  273.0 19.0 %copy-start.5 = (bf16[4,128,1536]{2,1,0:T(8,128)(2,1)S(1)}, bf16[4,128,1536]{2,1,0:T(8,128)(2,1)}, u32[]{:S(2)}) copy-start(bf16[4,128,1536]{2,1,0:T(8,128)(2,1)} %shard_map.124) | copy-start | bytes 4718596
  288.1 3.9 copy-start.14
  292.1 3.2 copy-start.4
  292.1 3.2 copy-start.16
  295.3 3.2 copy-start.6
  295.3 3.2 copy-start.9
  298.4 1.4 copy-start.3
  298.5 1.7 copy-start.8
where the time goes:
time: 448 us; the launch traced here: 443 us
  Pallas kernels  311 us (69%)
  matrix products  56.2 us (13%)
  other arithmetic  49.4 us (11%)
  local copies, waits for them, and re-layouts  25 us (6%)
    pallas_call x1, Pallas kernels, torus_gather(): pl.pallas_call(gather_kernel, out_shape=jax.ShapeDtypeStruct((4, 4, 2, RO...  89.6 us
    pallas_call x1, Pallas kernels, torus_scatter(): pl.pallas_call(scatter_kernel, out_shape=jax.ShapeDtypeStruct((ROWS, 3 *...  84.1 us
    pallas_call x4, Pallas kernels, seq_scatter(): pl.pallas_call(seq_scatter_kernel, out_shape=jax.ShapeDtypeStruct((own, w...  64.5 us
    pallas_call x4, Pallas kernels, seq_gather(): pl.pallas_call(seq_gather_kernel, out_shape=jax.ShapeDtypeStruct((4, own,...  61.9 us
    dot_general x12, matrix products, contract(): lax.dot_general(left, right, (((left_dim,), (right_dim,)), ((), ())), pre...  56.2 us
    concatenate x1, other arithmetic, local(): jnp.concatenate([grad_term(a1, dqkv), grad_term(da, attended), grad_term(...  32.6 us
    concatenate x1, local copies, waits for them, and re-layouts, local(): jnp.concatenate([grad_term(a1, dqkv), grad_term(da, attended), grad_term(...  18.8 us

commit v1 on v0

v1 whole, which is shorter than its diff:
```python
import functools
import math

import jax
import jax.numpy as jnp
from jax import lax
from jax.experimental import pallas as pl
from jax.experimental.pallas import tpu as pltpu
from jax.sharding import PartitionSpec as P

HEAD_DIM = 128
LN_EPS = 1e-06
TEMPER = 2.5
F32 = jnp.float32
BF16 = jnp.bfloat16
MESH = pl.DeviceIdType.MESH
GROUP = 1536
HALF = GROUP // 2
QUART = GROUP // 4
ROWS = 48


def rem(a, n):
    return lax.rem(a, n)


class Place:
    def __init__(self):
        f = lax.axis_index("fsdp")
        s = lax.axis_index("sp")
        self.z, self.y, self.xh = lax.div(f, 8), rem(lax.div(f, 2), 4), rem(f, 2)
        self.xl, self.c = lax.div(s, 2), rem(s, 2)
        self.s = s

    def dev(self, **kw):
        v = {k: kw.get(k, getattr(self, k)) for k in ("z", "y", "xh", "xl", "c")}
        return (v["z"] * 8 + v["y"] * 2 + v["xh"], v["xl"] * 2 + v["c"])

    def ring(self, axis, step):
        return rem(getattr(self, axis) + step + 4, 4)

    def near(self, axis, step):
        return self.dev(**{axis: self.ring(axis, step)})

    def across(self):
        return self.dev(xh=1 - self.xh)

    def chip(self):
        return self.dev(xl=1 - self.xl)

    def core(self):
        return self.dev(c=1 - self.c)


def greet(devices):
    barrier = pltpu.get_barrier_semaphore()
    for d in devices:
        pl.semaphore_signal(barrier, inc=1, device_id=d, device_id_type=MESH)
    pl.semaphore_wait(barrier, len(devices))


def torus_peers(me):
    return [me.near(a, s) for a in ("z", "y") for s in (1, -1)] + [me.across()]


class Sends:
    def __init__(self):
        self.open = []

    def start(self, src, dst, ssem, rsem, dev):
        copy = pltpu.make_async_remote_copy(
            src_ref=src, dst_ref=dst, send_sem=ssem, recv_sem=rsem, device_id=dev, device_id_type=MESH
        )
        copy.start()
        self.open.append(copy)

    def close(self):
        for copy in self.open:
            copy.wait_send()
        self.open = []


def arrive(ref, rsem, dev):
    pltpu.make_async_remote_copy(
        src_ref=ref, dst_ref=ref, send_sem=rsem, recv_sem=rsem, device_id=dev, device_id_type=MESH
    ).wait_recv()


class Gather:
    def __init__(self, me, w, half, col, xb, ssem, rsem, sends):
        self.me, self.w, self.xb, self.ssem, self.rsem, self.sends = me, w, xb, ssem, rsem, sends
        self.axes = ("y", "z") if half == 0 else ("z", "y")
        self.c0 = col + half * HALF

    def part(self, level, step, cols):
        axis = self.axes[level]
        at = {"z": self.me.z, "y": self.me.y}
        at[axis] = self.me.ring(axis, step)
        if level == 1:
            at[self.axes[0]] = slice(None)
        return self.w.at[at["z"], at["y"], self.xb, :, cols]

    def cols(self, which):
        return {
            "all": pl.ds(self.c0, HALF),
            "lo": pl.ds(self.c0, QUART),
            "hi": pl.ds(self.c0 + QUART, QUART),
        }[which]

    def go(self, level, step, which, to, i):
        ref = self.part(level, step, self.cols(which))
        i = level * 4 + i
        self.sends.start(ref, ref, self.ssem.at[i], self.rsem.at[i], self.me.near(self.axes[level], to))

    def got(self, level, step, which, i):
        arrive(self.part(level, step, self.cols(which)), self.rsem.at[level * 4 + i], self.me.near(self.axes[level], 1))

    def first(self, level):
        self.go(level, 0, "all", 1, 0)
        self.go(level, 0, "all", -1, 1)

    def second(self, level):
        self.got(level, -1, "all", 0)
        self.go(level, -1, "lo", 1, 2)
        self.got(level, 1, "all", 1)
        self.go(level, 1, "hi", -1, 3)

    def last(self, level):
        self.got(level, 2, "lo", 2)
        self.got(level, 2, "hi", 3)


def wider(ref_value):
    return ref_value.astype(F32)


def pack(total):
    return total.astype(BF16)


class Scatter:
    def __init__(self, me, g, half, xb, bufs, ssem, rsem, sends):
        self.me, self.g, self.xb, self.ssem, self.rsem, self.sends = me, g, xb, ssem, rsem, sends
        self.axes = ("z", "y") if half == 0 else ("y", "z")
        self.c0 = half * HALF
        self.bufs = bufs

    def spot(self, level, step, which):
        axis = self.axes[level]
        at = {"z": self.me.z, "y": self.me.y}
        at[axis] = self.me.ring(axis, step)
        if level == 0:
            at[self.axes[1]] = slice(None)
        cols = {
            "all": pl.ds(self.c0, HALF),
            "lo": pl.ds(self.c0, QUART),
            "hi": pl.ds(self.c0 + QUART, QUART),
        }[which]
        return (at["z"], at["y"], self.xb, slice(None), cols)

    def far(self, level):
        for to, which, i in ((1, "lo", 0), (-1, "hi", 1)):
            j = level * 4 + i
            self.sends.start(
                self.g.at[self.spot(level, 2, which)], self.bufs[level][0].at[i],
                self.ssem.at[j], self.rsem.at[j], self.me.near(self.axes[level], to),
            )

    def relay(self, level):
        for to, which, i in ((1, "lo", 0), (-1, "hi", 1)):
            buf = self.bufs[level][0].at[i]
            arrive(buf, self.rsem.at[level * 4 + i], self.me.near(self.axes[level], -to))
            spot = self.spot(level, to, which)
            self.g[spot] = (wider(self.g[spot]) + wider(buf[...])).astype(BF16)
        for to, i in ((1, 0), (-1, 1)):
            j = level * 4 + 2 + i
            self.sends.start(
                self.g.at[self.spot(level, to, "all")], self.bufs[level][1].at[i],
                self.ssem.at[j], self.rsem.at[j], self.me.near(self.axes[level], to),
            )

    def total(self, level):
        near = self.bufs[level][1]
        for to, i in ((1, 0), (-1, 1)):
            arrive(near.at[i], self.rsem.at[level * 4 + 2 + i], self.me.near(self.axes[level], -to))
        spot = self.spot(level, 0, "all")
        return spot, wider(self.g[spot]) + wider(near[0]) + wider(near[1])

    def fold(self):
        spot, total = self.total(0)
        self.g[spot] = total.astype(BF16)


DMA = pltpu.SemaphoreType.DMA
VM = pl.BlockSpec(memory_space=pltpu.VMEM)
OWN = 128
WIDTH = 1536
HEADS = 3
QKV = HEADS * HEAD_DIM
GELU_A = math.sqrt(2.0 / math.pi)
GELU_B = 0.044715


class SeqGather:
    def __init__(self, me, buf, ssem, rsem, sends):
        self.me, self.buf, self.ssem, self.rsem, self.sends = me, buf, ssem, rsem, sends

    def push(self, block, i, dev):
        self.sends.start(self.buf.at[block], self.buf.at[block], self.ssem.at[i], self.rsem.at[i], dev)

    def start(self):
        self.push(self.me.s, 0, self.me.chip())
        self.push(self.me.s, 1, self.me.core())

    def relay(self):
        other = (1 - self.me.xl) * 2 + self.me.c
        arrive(self.buf.at[other], self.rsem.at[0], self.me.chip())
        self.push(other, 2, self.me.core())

    def near(self):
        arrive(self.buf.at[self.me.xl * 2 + 1 - self.me.c], self.rsem.at[1], self.me.core())

    def far(self):
        arrive(self.buf.at[(1 - self.me.xl) * 2 + 1 - self.me.c], self.rsem.at[2], self.me.core())


class SeqScatter:
    def __init__(self, me, part, swap, mine, theirs, ssem, rsem):
        self.me, self.part, self.swap, self.mine, self.theirs = me, part, swap, mine, theirs
        self.ssem, self.rsem, self.sends = ssem, rsem, Sends()

    def give(self, i):
        xl = self.me.xl if i else 1 - self.me.xl
        self.sends.start(
            self.part.at[xl * 2 + 1 - self.me.c], self.swap.at[i], self.ssem.at[i], self.rsem.at[i], self.me.core()
        )

    def cross(self):
        arrive(self.swap.at[0], self.rsem.at[0], self.me.core())

        @pl.loop(0, 4)
        def _(i):
            r = pl.ds(i * 32, 32)
            self.mine[r] = pack(wider(self.part[(1 - self.me.xl) * 2 + self.me.c, r]) + wider(self.swap[0, r]))

        self.sends.start(self.mine, self.theirs, self.ssem.at[2], self.rsem.at[2], self.me.chip())

    def wait(self):
        arrive(self.swap.at[1], self.rsem.at[1], self.me.core())
        arrive(self.theirs, self.rsem.at[2], self.me.chip())

    def rows(self, r):
        return wider(self.part[self.me.s, r]) + wider(self.swap[1, r]) + wider(self.theirs[r])


def normalize(stream):
    centred = stream - jnp.mean(stream, axis=-1, keepdims=True)
    rstd = lax.rsqrt(jnp.mean(centred * centred, axis=-1, keepdims=True) + LN_EPS)
    return (centred * rstd, rstd)


def norm_back(normed, rstd, incoming):
    first = jnp.mean(incoming, axis=-1, keepdims=True)
    second = jnp.mean(incoming * normed, axis=-1, keepdims=True)
    return rstd * (incoming - first - normed * second)


def contract(left, right, left_dim, right_dim):
    return lax.dot_general(
        left, right, (((left_dim,), (right_dim,)), ((), ())), preferred_element_type=F32
    )


def softmax_rows(queries, key_rows, factor):
    scores = contract(queries, key_rows, 1, 1) * factor
    scores = jnp.exp(scores - jnp.max(scores, axis=-1, keepdims=True))
    return scores * (1.0 / jnp.sum(scores, axis=-1, keepdims=True))


def by_rows(body):
    @pl.loop(0, OWN // 32)
    def _(i):
        body(pl.ds(pl.multiple_of(i * 32, 32), 32))


def step_kernel(
    grad_scale, factor,
    tok, mod, blk, og,
    final, grad, oq, oo, oi, ob,
    w, g, r1, r2, p1, p2, xbuf, part, a1, a2, dm, da, packed, att, datt, act, slope, du,
    pa, pb, swaps, mines, theirs, middle,
    gs, gr, ss, rs, xs, xr, ys, yr, es, er, csem,
):
    me = Place()
    own = pltpu.make_async_copy(blk, w.at[me.z, me.y, me.xh], csem)
    own.start()
    greet(torus_peers(me) + [me.chip(), me.core()])
    own.wait()
    mine, other = me.xl, 1 - me.xl

    def m(i):
        return mod[pl.ds(i, 1), :]

    sends = Sends()
    pieces = []
    for group in range(3):
        for side in range(2):
            xb = me.xh if side == 0 else 1 - me.xh
            k = (group * 2 + side) * 2
            pieces.append([Gather(me, w, h, group * GROUP, xb, gs.at[k + h], gr.at[k + h], sends) for h in range(2)])

    def gather_event(k, what, level):
        if what == "first" and level == 0 and k % 2 == 1:
            arrive(w.at[me.z, me.y, 1 - me.xh, :, pl.ds(k // 2 * GROUP, GROUP)], xr.at[k // 2], me.across())
        for half in pieces[k]:
            getattr(half, what)(level)

    def cross(group):
        ref = w.at[me.z, me.y, me.xh, :, pl.ds(group * GROUP, GROUP)]
        sends.start(ref, ref, xs.at[group], xr.at[group], me.across())

    events = [(0, "first", 0), (0, "second", 0), (1, "first", 0), (0, "last", 0)]
    for k in range(7):
        events += [
            (k, "first", 1), (k + 2, "first", 0), (k + 1, "second", 0),
            (k - 1, "last", 1), (k, "second", 1), (k + 1, "last", 0),
        ]
    events = [e for e in events if 0 <= e[0] < 6]

    def ag(*upto):
        while events:
            event = events.pop(0)
            gather_event(*event)
            if event == upto:
                return

    scatters = []
    for n, group in enumerate((2, 1, 0)):
        for side in range(2):
            xb = 1 - me.xh if side == 0 else me.xh
            k = n * 2 + side
            halves = []
            for h in range(2):
                bufs = ((r1.at[k % 3, h], r2.at[k % 3, h]), (p1.at[k % 3, h], p2.at[k % 3, h]))
                halves.append(Scatter(me, g.at[group], h, xb, bufs, ss.at[k * 2 + h], rs.at[k * 2 + h], sends))
            scatters.append((group, side, halves))

    def slots(group, h):
        if group == 0:
            outs = ((oq.at[0], oq.at[1]), (oq.at[2], oo))[h]
            return [(outs[i], slice(i * QUART, (i + 1) * QUART)) for i in range(2)]
        ref = oi if group == 1 else ob
        return [(ref.at[:, pl.ds(h * HALF, HALF)], slice(0, HALF))]

    def finish(k):
        group, side, halves = scatters[k]
        cols = pl.ds(group * GROUP, GROUP)
        if side == 1:
            arrive(xbuf.at[:, cols], yr.at[group], me.across())
        for h, half in enumerate(halves):
            _, total = half.total(1)
            here = pl.ds(group * GROUP + h * HALF, HALF)
            if side == 0:
                part[:, here] = pack(total)
            else:
                total = total + wider(xbuf[:, here])
                for ref, sl in slots(group, h):
                    ref[...] = total[:, sl]
        if side == 0:
            sends.start(part.at[:, cols], xbuf.at[:, cols], ys.at[group], yr.at[group], me.across())

    def scatter_event(k, what, *args):
        if what == "finish":
            finish(k)
        else:
            for half in scatters[k][2]:
                getattr(half, what)(*args)

    reduce = [(0, "far", 0)]
    for t in range(9):
        reduce += [
            (t + 1, "far", 0), (t, "relay", 0), (t - 1, "fold"),
            (t - 1, "far", 1), (t - 2, "relay", 1), (t - 3, "finish"),
        ]
    reduce = [e for e in reduce if 0 <= e[0] < 6]

    def rsc(*upto):
        while reduce:
            event = reduce.pop(0)
            scatter_event(*event)
            if event == upto:
                return

    def rows_of(ref, side, cols=slice(None)):
        value = ref[pl.ds(side * 2, 2), :, cols]
        return value.reshape(2 * OWN, value.shape[-1])

    def forward(src, side, col, width, tile, emit):
        @pl.loop(0, width // tile)
        def _(j):
            at = pl.multiple_of(j * tile, 128)
            weight = w[:, :, :, :, pl.ds(col + at, tile)].reshape(WIDTH, tile)
            emit(pl.ds(at, tile), contract(rows_of(src, side), weight, 1, 0).reshape(2, OWN, tile))

    def backward(src, side, col, width, out):
        @pl.loop(0, 2)
        def _(j):
            weight = w[pl.ds(j * 2, 2), :, :, :, pl.ds(col, width)].reshape(HALF, width)
            at = pl.multiple_of(j * HALF, 128)
            value = contract(rows_of(src, side), weight, 1, 1)
            out[pl.ds(side * 2, 2), :, pl.ds(at, HALF)] = pack(value).reshape(2, OWN, HALF)

    def gradient(left, right, group, col, width):
        @pl.loop(0, 4)
        def _(j):
            rows = left[:, :, pl.ds(pl.multiple_of(j * 384, 128), 384)].reshape(4 * OWN, 384)
            value = contract(rows, right[...].reshape(4 * OWN, width), 0, 0) * grad_scale
            g[group, j, :, :, :, pl.ds(col, width)] = pack(value).reshape(4, 2, ROWS, width)

    gather = [SeqGather(me, buf, es.at[i], er.at[i], sends) for i, buf in enumerate((a1, a2, dm, da))]
    give = [
        SeqScatter(me, (pa, pa, pa, pb)[i], swaps.at[i // 3], mines.at[i // 3], theirs.at[i // 3], es.at[4 + i], er.at[4 + i])
        for i in range(4)
    ]
    x_a1, x_a2, x_dm, x_da = gather
    y_att, y_back, y_first, y_ffn = give

    def share(y, src, col, width, close=None):
        backward(src, other, col, width, y.part)
        y.give(0)
        backward(src, mine, col, width, y.part)
        y.give(1)
        y.cross()

    cross(0)
    ag(0, "first", 0)

    def first_norm(r):
        n1, _ = normalize(wider(tok[r]))
        a1[me.s, r] = pack(n1 * (1.0 + m(1)) + m(0))

    by_rows(first_norm)
    x_a1.start()
    cross(1)
    cross(2)

    def gate(r):
        dm[me.s, r] = pack(m(5) * wider(og[r]))

    by_rows(gate)
    ag(1, "second", 0)
    x_a1.relay()
    ag(2, "last", 0)
    x_a1.near()
    x_a1.far()
    x_dm.start()
    ag(1, "last", 1)

    def put_qkv(side):
        def emit(cols, value):
            packed[pl.ds(side * 2, 2), :, cols] = pack(value)
        return emit

    forward(a1, mine, 0, 3 * QKV, QKV, put_qkv(mine))
    forward(a1, other, 0, 3 * QKV, QKV, put_qkv(other))
    ag(5, "first", 0)
    x_dm.relay()

    def head_cols(place, head):
        return pl.ds(pl.multiple_of(place * QKV + head * HEAD_DIM, HEAD_DIM), HEAD_DIM)

    def head_rows(ref, cols):
        return ref[:, :, cols].reshape(4 * OWN, HEAD_DIM)

    @pl.loop(0, HEADS)
    def _(head):
        q, k, v = (head_rows(packed, head_cols(i, head)) for i in range(3))
        probs = softmax_rows(q, k, factor)
        att[:, :, head_cols(0, head)] = pack(contract(pack(probs), v, 1, 0)).reshape(4, OWN, HEAD_DIM)

    share(y_att, att, 3 * QKV, QKV)
    x_dm.near()
    x_dm.far()
    ag(4, "first", 1)
    y_att.wait()

    def second_norm(r):
        mid = wider(tok[r]) + m(2) * y_att.rows(r)
        middle[r] = mid
        n2, _ = normalize(mid)
        a2[me.s, r] = pack(n2 * (1.0 + m(4)) + m(3))

    by_rows(second_norm)
    y_att.sends.close()
    x_a2.start()
    ag(3, "last", 1)
    x_a2.near()

    def put_hidden(side):
        def emit(cols, u):
            t = jnp.tanh(GELU_A * (u + GELU_B * (u * u * u)))
            at = (pl.ds(side * 2, 2), slice(None), cols)
            act[at] = pack(0.5 * u * (1.0 + t))
            slope[at] = 0.5 * (1.0 + t) + (0.5 * GELU_A) * u * (1.0 - t * t) * (1.0 + (3.0 * GELU_B) * (u * u))
        return emit

    forward(a2, mine, GROUP, GROUP, 512, put_hidden(mine))
    ag(5, "first", 1)
    x_a2.relay()
    ag(4, "last", 1)
    x_a2.far()
    forward(a2, other, GROUP, GROUP, 512, put_hidden(other))
    ag(5, "second", 1)

    gradient(dm, act, 2, 0, GROUP)
    rsc(1, "far", 0)
    ag()

    def put_du(side):
        def emit(cols, dg):
            at = (pl.ds(side * 2, 2), slice(None), cols)
            du[at] = pack(slope[at] * dg)
        return emit

    forward(dm, other, 2 * GROUP, GROUP, 512, put_du(other))
    forward(dm, mine, 2 * GROUP, GROUP, 512, put_du(mine))
    share(y_back, du, GROUP, GROUP)
    rsc(0, "relay", 0)
    gradient(a2, du, 1, 0, GROUP)
    rsc(1, "relay", 0)
    y_back.wait()

    def middle_back(r):
        n2, rstd = normalize(middle[r])
        up = wider(og[r]) + norm_back(n2, rstd, y_back.rows(r) * (1.0 + m(4)))
        grad[r] = up
        da[me.s, r] = pack(m(2) * up)

    by_rows(middle_back)
    y_back.sends.close()
    x_da.start()
    rsc(3, "far", 0)
    backward(act, other, 2 * GROUP, GROUP, pb)
    backward(act, mine, 2 * GROUP, GROUP, pb)
    x_da.relay()
    x_da.near()
    y_ffn.give(0)
    y_ffn.give(1)

    def put_do(side):
        def emit(cols, value):
            datt[pl.ds(side * 2, 2), :, cols] = pack(value)
        return emit

    forward(da, mine, 3 * QKV, QKV, QKV, put_do(mine))
    x_da.far()
    y_ffn.cross()
    forward(da, other, 3 * QKV, QKV, QKV, put_do(other))
    rsc(2, "relay", 0)

    @pl.loop(0, HEADS)
    def _(head):
        q, k, v = (head_rows(packed, head_cols(i, head)) for i in range(3))
        up = head_rows(datt, head_cols(0, head))
        probs = softmax_rows(q, k, factor)
        dprobs = contract(up, v, 1, 1)
        dscores = pack(probs * (dprobs - jnp.sum(probs * dprobs, axis=-1, keepdims=True)) * factor)
        parts = (contract(dscores, k, 1, 0), contract(dscores, q, 0, 0), contract(pack(probs), up, 0, 0))
        for i, value in enumerate(parts):
            packed[:, :, head_cols(i, head)] = pack(value).reshape(4, OWN, HEAD_DIM)

    share(y_first, packed, 0, 3 * QKV)
    rsc(0, "relay", 1)
    gradient(a1, packed, 0, 0, 3 * QKV)
    gradient(da, att, 0, 3 * QKV, QKV)
    rsc(3, "relay", 0)
    y_ffn.wait()

    def last_out(r):
        final[r] = pack(middle[r] + m(5) * y_ffn.rows(r))

    by_rows(last_out)
    rsc(2, "far", 1)
    y_first.wait()

    def first_back(r):
        n1, rstd = normalize(wider(tok[r]))
        grad[r] = grad[r] + norm_back(n1, rstd, y_first.rows(r) * (1.0 + m(1)))

    by_rows(first_back)
    rsc()
    sends.close()
    y_first.sends.close()
    y_ffn.sends.close()


def local(tokens, modulation, w_qkv, w_out, w_in, w_back, out_grad):
    grad_scale = 1.0 / math.sqrt(OWN * lax.axis_size("sp") * lax.axis_size("fsdp"))
    factor = TEMPER / math.sqrt(HEAD_DIM)
    block = jnp.concatenate([w_qkv[0].reshape(ROWS, 3 * QKV), w_out[0].T, w_in[0], w_back[0].T], axis=1)

    def shape(dims, dtype=BF16):
        return jax.ShapeDtypeStruct(dims, dtype)

    def vm(*dims, dtype=BF16):
        return pltpu.VMEM(dims, dtype)

    seq = (4, OWN, WIDTH)
    final, grad, oq, oo, oi, ob = pl.pallas_call(
        functools.partial(step_kernel, grad_scale, factor),
        out_shape=(
            shape((OWN, WIDTH)), shape((OWN, WIDTH), F32), shape((3, ROWS, QKV), F32),
            shape((ROWS, QKV), F32), shape((ROWS, GROUP), F32), shape((ROWS, GROUP), F32),
        ),
        in_specs=[VM] * 4,
        out_specs=(VM,) * 6,
        scratch_shapes=[
            vm(4, 4, 2, ROWS, 3 * GROUP), vm(3, 4, 4, 2, ROWS, GROUP),
            vm(3, 2, 2, 4, ROWS, QUART), vm(3, 2, 2, 4, ROWS, HALF),
            vm(3, 2, 2, ROWS, QUART), vm(3, 2, 2, ROWS, HALF),
            vm(ROWS, 3 * GROUP), vm(ROWS, 3 * GROUP),
            vm(*seq), vm(*seq), vm(*seq), vm(*seq),
            vm(4, OWN, 3 * QKV), vm(4, OWN, QKV), vm(4, OWN, QKV),
            vm(*seq), vm(*seq, dtype=F32), vm(*seq),
            vm(*seq), vm(*seq), vm(2, 2, OWN, WIDTH), vm(2, OWN, WIDTH), vm(2, OWN, WIDTH),
            vm(OWN, WIDTH, dtype=F32),
            DMA((12, 8)), DMA((12, 8)), DMA((12, 8)), DMA((12, 8)),
            DMA((3,)), DMA((3,)), DMA((3,)), DMA((3,)), DMA((8, 3)), DMA((8, 3)), DMA,
        ],
        compiler_params=pltpu.CompilerParams(
            collective_id=0, has_side_effects=True, vmem_limit_bytes=67043328
        ),
    )(tokens[0], modulation[0, 0], block, out_grad[0])
    return (
        final[None], grad[None], oq.transpose(1, 0, 2)[None], oo.T[None], oi[None], ob.T[None],
    )


def solution(mesh):
    weights = (
        P(None, "fsdp", None, "sp"),
        P(None, "sp", "fsdp"),
        P(None, "fsdp", "sp"),
        P(None, "sp", "fsdp"),
    )
    rows = P("fsdp", "sp", None)
    return jax.shard_map(
        local,
        mesh=mesh,
        in_specs=(rows, P("fsdp", None, None, None), *weights, rows),
        out_specs=(rows, rows, *weights),
        check_vma=False,
    )
```

time: 448 us -> 195 us (0.44)
  Pallas kernels: 311 us -> 181 us
  matrix products: 56.2 us -> 0 us
  other arithmetic: 49.4 us -> 0.79 us
  local copies, waits for them, and re-layouts: 25 us -> 9.58 us
    pallas_call x12 -> x1, Pallas kernels: 311 us -> 181 us  [local(): pl.pallas_call(functools.partial(step_kernel, grad_scale, factor), out_sh...]
    dot_general x12 -> x0, matrix products: 56.2 us -> none  [contract(): lax.dot_general(left, right, (((left_dim,), (right_dim,)), ((), ())), pre...]
    concatenate x2 -> x1, other arithmetic: 33.4 us -> 0.79 us  [local(): jnp.concatenate([w_qkv[0].reshape(ROWS, 3 * QKV), w_out[0].T, w_in[0], w_...]
    concatenate x1 -> x0, local copies, waits for them, and re-layouts: 18.8 us -> none  [local(): jnp.concatenate([grad_term(a1, dqkv), grad_term(da, attended), grad_term(...]
    unnamed x37 -> x25, local copies, waits for them, and re-layouts: 1.73 us -> 9.58 us
    reduce_sum x6 -> x0, other arithmetic: 6.9 us -> none  [the longest x2 2.96 us: norm_back(): first = jnp.mean(incoming, axis=-1, keepdims=True)]
    convert_element_type x3 -> x0, other arithmetic: 5.78 us -> none  [the longest x1 2.52 us: local(): da = seq_gather((mod[2] * grad).astype(BF16), 8)]
where the time goes in v1:
time: 195 us; the launch traced here: 193 us
  Pallas kernels  181 us (93%)
  local copies, waits for them, and re-layouts  9.58 us (5%)
    pallas_call x1, Pallas kernels, local(): pl.pallas_call(functools.partial(step_kernel, grad_scale, factor), out_sh...  181 us
    unnamed x25, local copies, waits for them, and re-layouts  9.58 us

profile of v1, /device:TPU:1, one launch (start us, length us, event | category | flops | bytes accessed | tf_op | source)
XLA Modules:
  0.0 192.5 jit_solution(5779144288366305953)
XLA Ops:
  0.6 1.4 copy.18
  2.0 0.0 copy-start.5
  2.0 1.0 copy.14
  3.0 0.0 copy-start.4
  3.0 0.0 copy-start.7
  3.1 0.0 copy-done.5
  3.1 0.9 copy-done.4
  3.9 0.0 copy-done.7
  3.9 0.8 pad_maximum_fusion.blk
  4.7 181.4 %shard_map.118 = (bf16[128,1536]{1,0:T(8,128)(2,1)}, f32[128,1536]{1,0:T(8,128)}, f32[3,48,384]{2,1,0:T(8,128)}, f32[48,384]{1,0:T(8,128)}, f32[48,1536]{1,0:T(8,128)}, /*index=5*/f32[48,1536]{1,0:T(8,128)}) custom-call(bf16[128,1536]{1,0:T(8,128)(2,1)} %bitcast.31, f32[6,1536]{1,0:T(8,128)} %bitcast.36, bf16[48,4608]{1,0:T(8,128)(2,1)} %pad_maximum_fusion.blk, ...), custom_call_target="tpu_custom_call" | custom-call | tf_op jit(solution)/shard_map/pallas_call | solution.py:609
  186.2 0.0 copy-start
  186.2 1.8 copy.25
  188.0 0.0 copy-done
  188.0 0.0 copy-start.3
  188.0 0.9 copy.26
  188.9 0.3 copy-done.3
  189.2 0.0 copy-start.6
  189.2 0.7 copy.27
  189.9 0.2 copy-done.6
  190.1 0.6 copy.28
  190.7 0.0 copy-done.2
  190.7 0.7 copy.29
  191.4 0.4 copy-done.1
  191.8 0.7 copy.30
  (3 shorter events, 0.0 us)
Async XLA Ops:
  2.0 1.0 copy-start.5
  3.0 0.9 copy-start.4
  3.0 0.9 copy-start.7
  186.2 1.9 copy-start
  188.0 1.1 copy-start.3
  189.2 0.9 copy-start.6
  189.2 1.5 copy-start.2
  190.7 1.1 copy-start.1

commit v2 on v1

v2 whole, which is shorter than its diff:
```python
import functools
import math

import jax
import jax.numpy as jnp
from jax import lax
from jax.experimental import pallas as pl
from jax.experimental.pallas import tpu as pltpu
from jax.sharding import PartitionSpec as P

HEAD_DIM = 128
LN_EPS = 1e-06
TEMPER = 2.5
F32 = jnp.float32
BF16 = jnp.bfloat16
MESH = pl.DeviceIdType.MESH
GROUP = 1536
HALF = GROUP // 2
QUART = GROUP // 4
ROWS = 48


def rem(a, n):
    return lax.rem(a, n)


class Place:
    def __init__(self):
        f = lax.axis_index("fsdp")
        s = lax.axis_index("sp")
        self.z, self.y, self.xh = lax.div(f, 8), rem(lax.div(f, 2), 4), rem(f, 2)
        self.xl, self.c = lax.div(s, 2), rem(s, 2)
        self.s = s
        self.x = self.xh * 2 + self.xl
        self.n = self.x * 2 + self.c

    def dev(self, **kw):
        v = {k: kw.get(k, getattr(self, k)) for k in ("z", "y", "xh", "xl", "c")}
        return (v["z"] * 8 + v["y"] * 2 + v["xh"], v["xl"] * 2 + v["c"])

    def ring(self, axis, step):
        return rem(getattr(self, axis) + step + 4, 4)

    def near(self, axis, step):
        return self.dev(**{axis: self.ring(axis, step)})

    def along(self, step):
        x = rem(self.x + step + 4, 4)
        return self.dev(xh=lax.div(x, 2), xl=rem(x, 2))

    def chip_at(self, step):
        return rem(self.x + step + 4, 4)

    def across(self):
        return self.dev(xh=1 - self.xh)

    def chip(self):
        return self.dev(xl=1 - self.xl)

    def core(self):
        return self.dev(c=1 - self.c)


def greet(devices):
    barrier = pltpu.get_barrier_semaphore()
    for d in devices:
        pl.semaphore_signal(barrier, inc=1, device_id=d, device_id_type=MESH)
    pl.semaphore_wait(barrier, len(devices))


def torus_peers(me):
    return [me.near(a, s) for a in ("z", "y") for s in (1, -1)] + [me.across(), me.along(1), me.along(-1), me.core()]


class Sends:
    def __init__(self):
        self.open = []

    def start(self, src, dst, ssem, rsem, dev):
        copy = pltpu.make_async_remote_copy(
            src_ref=src, dst_ref=dst, send_sem=ssem, recv_sem=rsem, device_id=dev, device_id_type=MESH
        )
        copy.start()
        self.open.append(copy)

    def close(self):
        for copy in self.open:
            copy.wait_send()
        self.open = []


def arrive(ref, rsem, dev):
    pltpu.make_async_remote_copy(
        src_ref=ref, dst_ref=ref, send_sem=rsem, recv_sem=rsem, device_id=dev, device_id_type=MESH
    ).wait_recv()


class Gather:
    def __init__(self, me, w, half, col, xb, ssem, rsem, sends):
        self.me, self.w, self.xb, self.ssem, self.rsem, self.sends = me, w, xb, ssem, rsem, sends
        self.axes = ("y", "z") if half == 0 else ("z", "y")
        self.c0 = col + half * HALF

    def part(self, level, step, cols):
        axis = self.axes[level]
        at = {"z": self.me.z, "y": self.me.y}
        at[axis] = self.me.ring(axis, step)
        if level == 1:
            at[self.axes[0]] = slice(None)
        return self.w.at[at["z"], at["y"], self.xb, :, cols]

    def cols(self, which):
        return {
            "all": pl.ds(self.c0, HALF),
            "lo": pl.ds(self.c0, QUART),
            "hi": pl.ds(self.c0 + QUART, QUART),
        }[which]

    def go(self, level, step, which, to, i):
        ref = self.part(level, step, self.cols(which))
        i = level * 4 + i
        self.sends.start(ref, ref, self.ssem.at[i], self.rsem.at[i], self.me.near(self.axes[level], to))

    def got(self, level, step, which, i):
        arrive(self.part(level, step, self.cols(which)), self.rsem.at[level * 4 + i], self.me.near(self.axes[level], 1))

    def first(self, level):
        self.go(level, 0, "all", 1, 0)
        self.go(level, 0, "all", -1, 1)

    def second(self, level):
        self.got(level, -1, "all", 0)
        self.go(level, -1, "lo", 1, 2)
        self.got(level, 1, "all", 1)
        self.go(level, 1, "hi", -1, 3)

    def last(self, level):
        self.got(level, 2, "lo", 2)
        self.got(level, 2, "hi", 3)


def wider(ref_value):
    return ref_value.astype(F32)


def pack(total):
    return total.astype(BF16)


class Scatter:
    def __init__(self, me, g, half, xb, bufs, ssem, rsem, sends):
        self.me, self.g, self.xb, self.ssem, self.rsem, self.sends = me, g, xb, ssem, rsem, sends
        self.axes = ("z", "y") if half == 0 else ("y", "z")
        self.c0 = half * HALF
        self.bufs = bufs

    def spot(self, level, step, which):
        axis = self.axes[level]
        at = {"z": self.me.z, "y": self.me.y}
        at[axis] = self.me.ring(axis, step)
        if level == 0:
            at[self.axes[1]] = slice(None)
        cols = {
            "all": pl.ds(self.c0, HALF),
            "lo": pl.ds(self.c0, QUART),
            "hi": pl.ds(self.c0 + QUART, QUART),
        }[which]
        return (at["z"], at["y"], self.xb, slice(None), cols)

    def far(self, level):
        for to, which, i in ((1, "lo", 0), (-1, "hi", 1)):
            j = level * 4 + i
            self.sends.start(
                self.g.at[self.spot(level, 2, which)], self.bufs[level][0].at[i],
                self.ssem.at[j], self.rsem.at[j], self.me.near(self.axes[level], to),
            )

    def relay(self, level):
        for to, which, i in ((1, "lo", 0), (-1, "hi", 1)):
            buf = self.bufs[level][0].at[i]
            arrive(buf, self.rsem.at[level * 4 + i], self.me.near(self.axes[level], -to))
            spot = self.spot(level, to, which)
            self.g[spot] = (wider(self.g[spot]) + wider(buf[...])).astype(BF16)
        for to, i in ((1, 0), (-1, 1)):
            j = level * 4 + 2 + i
            self.sends.start(
                self.g.at[self.spot(level, to, "all")], self.bufs[level][1].at[i],
                self.ssem.at[j], self.rsem.at[j], self.me.near(self.axes[level], to),
            )

    def total(self, level):
        near = self.bufs[level][1]
        for to, i in ((1, 0), (-1, 1)):
            arrive(near.at[i], self.rsem.at[level * 4 + 2 + i], self.me.near(self.axes[level], -to))
        spot = self.spot(level, 0, "all")
        return spot, wider(self.g[spot]) + wider(near[0]) + wider(near[1])

    def fold(self):
        spot, total = self.total(0)
        self.g[spot] = total.astype(BF16)


DMA = pltpu.SemaphoreType.DMA
VM = pl.BlockSpec(memory_space=pltpu.VMEM)
ANY = pl.BlockSpec(memory_space=pl.ANY)
OWN = 128
WIDTH = 1536
HEADS = 3
QKV = HEADS * HEAD_DIM
GELU_A = math.sqrt(2.0 / math.pi)
GELU_B = 0.044715


class SeqGather:
    def __init__(self, me, buf, ssem, rsem, sends):
        self.me, self.buf, self.ssem, self.rsem, self.sends = me, buf, ssem, rsem, sends

    def push(self, block, i, dev):
        self.sends.start(self.buf.at[block], self.buf.at[block], self.ssem.at[i], self.rsem.at[i], dev)

    def start(self):
        self.push(self.me.s, 0, self.me.chip())
        self.push(self.me.s, 1, self.me.core())

    def relay(self):
        other = (1 - self.me.xl) * 2 + self.me.c
        arrive(self.buf.at[other], self.rsem.at[0], self.me.chip())
        self.push(other, 2, self.me.core())

    def near(self):
        arrive(self.buf.at[self.me.xl * 2 + 1 - self.me.c], self.rsem.at[1], self.me.core())

    def far(self):
        arrive(self.buf.at[(1 - self.me.xl) * 2 + 1 - self.me.c], self.rsem.at[2], self.me.core())


class SeqScatter:
    def __init__(self, me, part, swap, mine, theirs, ssem, rsem):
        self.me, self.part, self.swap, self.mine, self.theirs = me, part, swap, mine, theirs
        self.ssem, self.rsem, self.sends = ssem, rsem, Sends()

    def give(self, i):
        xl = self.me.xl if i else 1 - self.me.xl
        self.sends.start(
            self.part.at[xl * 2 + 1 - self.me.c], self.swap.at[i], self.ssem.at[i], self.rsem.at[i], self.me.core()
        )

    def cross(self):
        arrive(self.swap.at[0], self.rsem.at[0], self.me.core())

        @pl.loop(0, 4)
        def _(i):
            r = pl.ds(i * 32, 32)
            self.mine[r] = pack(wider(self.part[(1 - self.me.xl) * 2 + self.me.c, r]) + wider(self.swap[0, r]))

        self.sends.start(self.mine, self.theirs, self.ssem.at[2], self.rsem.at[2], self.me.chip())

    def wait(self):
        arrive(self.swap.at[1], self.rsem.at[1], self.me.core())
        arrive(self.theirs, self.rsem.at[2], self.me.chip())

    def rows(self, r):
        return wider(self.part[self.me.s, r]) + wider(self.swap[1, r]) + wider(self.theirs[r])


LEFT, RIGHT = pl.ds(0, HALF), pl.ds(HALF, HALF)


class RingGather:
    def __init__(self, me, buf, ssem, rsem, sends):
        self.me, self.buf, self.ssem, self.rsem, self.sends = me, buf, ssem, rsem, sends

    def at(self, step, mine=True, cols=pl.ds(0, WIDTH)):
        return self.buf.at[self.me.chip_at(step) * 2 + (self.me.c if mine else 1 - self.me.c), :, cols]

    def push(self, ref, i, dev):
        self.sends.start(ref, ref, self.ssem.at[i], self.rsem.at[i], dev)

    def start(self):
        self.push(self.at(0), 0, self.me.along(1))
        self.push(self.at(0), 1, self.me.along(-1))
        self.push(self.at(0), 2, self.me.core())

    def relay(self):
        for step, cols, i in ((-1, LEFT, 0), (1, RIGHT, 1)):
            arrive(self.at(step), self.rsem.at[i], self.me.core())
            self.push(self.at(step, cols=cols), 3 + i, self.me.along(-step))
            self.push(self.at(step), 5 + i, self.me.core())

    def last(self):
        for cols, i in ((LEFT, 0), (RIGHT, 1)):
            arrive(self.at(2, cols=cols), self.rsem.at[3 + i], self.me.core())
            self.push(self.at(2, cols=cols), 7 + i, self.me.core())

    def own(self):
        arrive(self.at(0, False), self.rsem.at[2], self.me.core())

    def sides(self):
        for step, i in ((-1, 5), (1, 6)):
            arrive(self.at(step, False), self.rsem.at[i], self.me.core())

    def far(self):
        for cols, i in ((LEFT, 7), (RIGHT, 8)):
            arrive(self.at(2, False, cols), self.rsem.at[i], self.me.core())


class RingScatter:
    order = (2, 1, -1, 0)

    def __init__(self, me, part, swap, away, near, ssem, rsem):
        self.me, self.part, self.swap, self.away, self.near = me, part, swap, away, near
        self.ssem, self.rsem, self.sends = ssem, rsem, Sends()

    def block(self, step):
        return self.me.chip_at(step) * 2 + self.me.c

    def give(self, j):
        src = self.part.at[self.me.chip_at(self.order[j]) * 2 + 1 - self.me.c]
        self.sends.start(src, self.swap.at[j], self.ssem.at[j], self.rsem.at[j], self.me.core())

    def out(self):
        arrive(self.swap.at[0], self.rsem.at[0], self.me.core())
        block = self.block(2)

        def merge(r):
            self.part[block, r] = pack(wider(self.part[block, r]) + wider(self.swap[0, r]))

        by_rows(merge)
        for cols, step, i in ((LEFT, 1, 0), (RIGHT, -1, 1)):
            self.sends.start(
                self.part.at[block, :, cols], self.away.at[i], self.ssem.at[4 + i], self.rsem.at[4 + i], self.me.along(step)
            )

    def relay(self):
        for step, j, i, same, rest in ((1, 1, 0, LEFT, RIGHT), (-1, 2, 1, RIGHT, LEFT)):
            arrive(self.swap.at[j], self.rsem.at[j], self.me.core())
            arrive(self.away.at[i], self.rsem.at[4 + i], self.me.core())
            block = self.block(step)

            def merge(r):
                both = wider(self.part[block, r, same]) + wider(self.swap[j, r, same])
                self.part[block, r, same] = pack(both + wider(self.away[i, r]))
                self.part[block, r, rest] = pack(wider(self.part[block, r, rest]) + wider(self.swap[j, r, rest]))

            by_rows(merge)
            self.sends.start(
                self.part.at[block], self.near.at[i], self.ssem.at[6 + i], self.rsem.at[6 + i], self.me.along(step)
            )

    def wait(self):
        arrive(self.swap.at[3], self.rsem.at[3], self.me.core())
        for i in range(2):
            arrive(self.near.at[i], self.rsem.at[6 + i], self.me.core())

    def rows(self, r):
        own = wider(self.part[self.block(0), r]) + wider(self.swap[3, r])
        return own + (wider(self.near[0, r]) + wider(self.near[1, r]))


def normalize(stream):
    centred = stream - jnp.mean(stream, axis=-1, keepdims=True)
    rstd = lax.rsqrt(jnp.mean(centred * centred, axis=-1, keepdims=True) + LN_EPS)
    return (centred * rstd, rstd)


def norm_back(normed, rstd, incoming):
    first = jnp.mean(incoming, axis=-1, keepdims=True)
    second = jnp.mean(incoming * normed, axis=-1, keepdims=True)
    return rstd * (incoming - first - normed * second)


def contract(left, right, left_dim, right_dim):
    return lax.dot_general(
        left, right, (((left_dim,), (right_dim,)), ((), ())), preferred_element_type=F32
    )


def softmax_rows(queries, key_rows, factor):
    scores = contract(queries, key_rows, 1, 1) * factor
    scores = jnp.exp(scores - jnp.max(scores, axis=-1, keepdims=True))
    return scores * (1.0 / jnp.sum(scores, axis=-1, keepdims=True))


def by_rows(body):
    @pl.loop(0, OWN // 32)
    def _(i):
        body(pl.ds(pl.multiple_of(i * 32, 32), 32))


def step_kernel(
    grad_scale, factor,
    tok, mod, wq, wo, wi, wb, og,
    final, grad, oq, oo, oi, ob,
    wa, wf, ga, gf, r1, r2, p1, p2, xbuf, part, partf, a1, a2, dm, da, packed, att, datt, act, slope, du,
    pa, pf, swap, own_sum, theirs, swapf, away, near, middle,
    gs, gr, ss, rs, xs, xr, ys, yr, es, er, csem,
):
    me = Place()
    mine_f = pl.multiple_of(me.xh * HALF, HALF)
    other_f = pl.multiple_of((1 - me.xh) * HALF, HALF)
    home_a, home_f = wa.at[me.z, me.y, me.xh], wf.at[me.z, me.y, me.xh]
    parts = [(wq.at[j], home_a.at[:, pl.ds(j * QKV, QKV)]) for j in range(3)] + [
        (wo, home_a.at[:, pl.ds(3 * QKV, QKV)]),
        (wi.at[:, pl.ds(mine_f, HALF)], home_f.at[:, LEFT]),
        (wb.at[:, pl.ds(mine_f, HALF)], home_f.at[:, RIGHT]),
    ]
    loads = [pltpu.make_async_copy(src, dst, csem.at[i]) for i, (src, dst) in enumerate(parts)]
    for load in loads:
        load.start()
    greet(torus_peers(me))
    for load in loads:
        load.wait()
    mine, other = me.xl, 1 - me.xl

    def m(i):
        return mod[i]

    sends = Sends()
    pieces = []
    for group, ref in enumerate((wa, wf)):
        for side in range(2):
            xb = me.xh if side == 0 else 1 - me.xh
            k = (group * 2 + side) * 2
            pieces.append([Gather(me, ref, h, 0, xb, gs.at[k + h], gr.at[k + h], sends) for h in range(2)])

    def gather_event(k, what, level):
        if what == "first" and level == 0 and k == 1:
            arrive(wa.at[me.z, me.y, 1 - me.xh], xr.at[0], me.across())
        if what == "first" and level == 0 and k == 3:
            for i, cols in ((1, LEFT), (2, RIGHT)):
                arrive(wf.at[me.z, me.y, 1 - me.xh, :, cols], xr.at[i], me.across())
        for half in pieces[k]:
            getattr(half, what)(level)

    def cross(group):
        if group == 0:
            sends.start(home_a, home_a, xs.at[0], xr.at[0], me.across())
        else:
            for i, ref, cols in ((1, wi, LEFT), (2, wb, RIGHT)):
                sends.start(ref.at[:, pl.ds(other_f, HALF)], home_f.at[:, cols], xs.at[i], xr.at[i], me.across())

    def ag(*steps):
        for step in steps:
            what = {"f": "first", "s": "second", "l": "last"}[step[0]]
            gather_event(int(step[2]), what, int(step[1]))

    scatters = []
    for n, ref in enumerate((gf, ga)):
        for side in range(2):
            xb = 1 - me.xh if side == 0 else me.xh
            k = n * 2 + side
            halves = []
            for h in range(2):
                bufs = ((r1.at[k, h], r2.at[k, h]), (p1.at[k, h], p2.at[k, h]))
                halves.append(Scatter(me, ref, h, xb, bufs, ss.at[k * 2 + h], rs.at[k * 2 + h], sends))
            scatters.append(halves)

    def finish(k, h):
        _, total = scatters[k][h].total(1)
        if k < 2:
            out = (oi, ob)[h]
            if k == 0:
                partf[h] = total
                sends.start(partf.at[h], out.at[:, pl.ds(mine_f, HALF)], ys.at[h], yr.at[h], me.across())
            else:
                out[:, pl.ds(mine_f, HALF)] = total
        elif k == 2:
            part[h] = pack(total)
            sends.start(part.at[h], xbuf.at[h], ys.at[2 + h], yr.at[2 + h], me.across())
        else:
            arrive(xbuf.at[h], yr.at[2 + h], me.across())
            total = total + wider(xbuf[h])
            outs = ((oq.at[0], oq.at[1]), (oq.at[2], oo))[h]
            for i, out in enumerate(outs):
                out[...] = total[:, i * QUART : (i + 1) * QUART]

    def rsc(*steps):
        names = {"f": ("far", 0), "r": ("relay", 0), "d": ("fold",), "g": ("far", 1), "s": ("relay", 1)}
        for step in steps:
            k = int(step[1])
            for h in (0, 1) if len(step) == 2 else (int(step[2]),):
                scatter_event(step, k, h, names)

    def scatter_event(step, k, h, names):
        if step[0] == "e":
            finish(k, h)
        else:
            name, *args = names[step[0]]
            getattr(scatters[k][h], name)(*args)

    def rows_of(ref, side, cols=slice(None)):
        value = ref[pl.ds(side * 2, 2), :, cols]
        return value.reshape(2 * OWN, value.shape[-1])

    def forward(src, side, w, col, width, emit):
        weight = w[:, :, :, :, pl.ds(col, width)].reshape(WIDTH, width)
        emit(contract(rows_of(src, side), weight, 1, 0).reshape(2, OWN, width))

    def backward(src, side, w, col, width, out):
        @pl.loop(0, 2)
        def _(j):
            weight = w[pl.ds(j * 2, 2), :, :, :, pl.ds(col, width)].reshape(HALF, width)
            at = pl.multiple_of(j * HALF, 128)
            value = contract(rows_of(src, side), weight, 1, 1)
            out[pl.ds(side * 2, 2), :, pl.ds(at, HALF)] = pack(value).reshape(2, OWN, HALF)

    def gradient(left, right, g, col, width):
        count = left.shape[0] * OWN

        @pl.loop(0, 4)
        def _(j):
            rows = left[:, :, pl.ds(pl.multiple_of(j * 384, 128), 384)].reshape(count, 384)
            value = contract(rows, right[...].reshape(count, width), 0, 0) * grad_scale
            g[j, :, :, :, pl.ds(col, width)] = pack(value).reshape(4, 2, ROWS, width)

    x_a1 = SeqGather(me, a1, es.at[0], er.at[0], sends)
    x_da = SeqGather(me, da, es.at[1], er.at[1], sends)
    x_a2 = RingGather(me, a2, es.at[2], er.at[2], sends)
    x_dm = RingGather(me, dm, es.at[3], er.at[3], sends)
    y_att = SeqScatter(me, pa, swap, own_sum, theirs, es.at[4], er.at[4])
    y_first = SeqScatter(me, pa, swap, own_sum, theirs, es.at[5], er.at[5])
    y_back = RingScatter(me, pf, swapf, away.at[0], near.at[0], es.at[6], er.at[6])
    y_ffn = RingScatter(me, pf, swapf, away.at[1], near.at[1], es.at[7], er.at[7])

    def share(y, src, col, width):
        backward(src, other, wa, col, width, y.part)
        y.give(0)
        backward(src, mine, wa, col, width, y.part)
        y.give(1)
        y.cross()

    def first_norm(r):
        n1, _ = normalize(wider(tok[r]))
        a1[me.s, r] = pack(n1 * (1.0 + m(1)) + m(0))

    def gate(r):
        dm[me.n, r] = pack(m(5) * wider(og[r]))

    def put(dst, side):
        def emit(value):
            dst[pl.ds(side * 2, 2)] = pack(value)
        return emit

    def head_cols(place, head):
        return pl.ds(pl.multiple_of(place * QKV + head * HEAD_DIM, HEAD_DIM), HEAD_DIM)

    def head_rows(ref, cols):
        return ref[:, :, cols].reshape(4 * OWN, HEAD_DIM)

    def attend(head):
        q, k, v = (head_rows(packed, head_cols(i, head)) for i in range(3))
        probs = softmax_rows(q, k, factor)
        att[:, :, head_cols(0, head)] = pack(contract(pack(probs), v, 1, 0)).reshape(4, OWN, HEAD_DIM)

    def attend_back(head):
        q, k, v = (head_rows(packed, head_cols(i, head)) for i in range(3))
        up = head_rows(datt, head_cols(0, head))
        probs = softmax_rows(q, k, factor)
        dprobs = contract(up, v, 1, 1)
        dscores = pack(probs * (dprobs - jnp.sum(probs * dprobs, axis=-1, keepdims=True)) * factor)
        parts = (contract(dscores, k, 1, 0), contract(dscores, q, 0, 0), contract(pack(probs), up, 0, 0))
        for i, value in enumerate(parts):
            packed[:, :, head_cols(i, head)] = pack(value).reshape(4, OWN, HEAD_DIM)

    def heads(body):
        pl.loop(0, HEADS)(body)

    def second_norm(r):
        mid = wider(tok[r]) + m(2) * y_att.rows(r)
        middle[r] = mid
        n2, _ = normalize(mid)
        a2[me.n, r] = pack(n2 * (1.0 + m(4)) + m(3))

    def hidden(chip):
        def emit(u):
            t = jnp.tanh(GELU_A * (u + GELU_B * (u * u * u)))
            at = pl.ds(chip * 2, 2)
            act[at] = pack(0.5 * u * (1.0 + t))
            slope[at] = 0.5 * (1.0 + t) + (0.5 * GELU_A) * u * (1.0 - t * t) * (1.0 + (3.0 * GELU_B) * (u * u))
        forward(a2, chip, wf, 0, HALF, emit)

    def hidden_back(step):
        chip = me.chip_at(step)

        def emit(dg):
            at = pl.ds(chip * 2, 2)
            du[at] = pack(slope[at] * dg)
        forward(dm, chip, wf, HALF, HALF, emit)

    def middle_back(r):
        n2, rstd = normalize(middle[r])
        up = wider(og[r]) + norm_back(n2, rstd, y_back.rows(r) * (1.0 + m(4)))
        grad[r] = up
        da[me.s, r] = pack(m(2) * up)

    def last_out(r):
        final[r] = pack(middle[r] + m(5) * y_ffn.rows(r))

    def first_back(r):
        n1, rstd = normalize(wider(tok[r]))
        grad[r] = grad[r] + norm_back(n1, rstd, y_first.rows(r) * (1.0 + m(1)))

    def sides(i):
        hidden(me.chip_at(2 * i - 1))

    cross(0)
    ag("f00", "f02")
    by_rows(first_norm)
    x_a1.start()
    cross(1)
    by_rows(gate)
    ag("s00", "f01", "l00", "f10", "s01", "s02")
    x_a1.relay()
    ag("l01", "f11", "s10", "l02", "f03", "s11", "f12", "s03")
    x_a1.near()
    x_a1.far()
    x_dm.start()
    ag("l10", "l03", "l11")
    forward(a1, mine, wa, 0, 3 * QKV, put(packed, mine))
    forward(a1, other, wa, 0, 3 * QKV, put(packed, other))
    ag("f13")
    heads(attend)
    share(y_att, att, 3 * QKV, QKV)
    ag("s12")
    x_dm.relay()
    ag("s13")
    x_dm.last()
    y_att.wait()
    by_rows(second_norm)
    y_att.sends.close()
    x_a2.start()
    x_dm.own()
    x_dm.sides()
    x_dm.far()
    ag("l12", "l13")
    x_a2.own()
    hidden(me.x)
    x_a2.relay()
    x_a2.sides()
    pl.loop(0, 2)(sides)
    x_a2.last()
    x_a2.far()
    hidden(me.chip_at(2))

    pl.loop(0, 4)(hidden_back)
    backward(du, me.chip_at(2), wf, 0, HALF, pf)
    y_back.give(0)
    backward(du, me.chip_at(1), wf, 0, HALF, pf)
    y_back.give(1)
    y_back.out()
    backward(du, me.chip_at(-1), wf, 0, HALF, pf)
    y_back.give(2)
    backward(du, me.chip_at(0), wf, 0, HALF, pf)
    y_back.give(3)
    gradient(dm, act, gf, HALF, HALF)
    rsc("f01", "f11")
    y_back.relay()
    gradient(a2, du, gf, 0, HALF)
    rsc("f00", "f10", "r01", "r11")
    rsc("r00", "r10")
    y_back.wait()
    by_rows(middle_back)
    y_back.sends.close()
    x_da.start()
    rsc("d01", "g01", "d11", "g11")
    backward(act, me.chip_at(2), wf, HALF, HALF, pf)
    backward(act, me.chip_at(1), wf, HALF, HALF, pf)
    rsc("d00", "g00", "d10", "g10", "s01", "s11")
    backward(act, me.chip_at(-1), wf, HALF, HALF, pf)
    backward(act, me.chip_at(0), wf, HALF, HALF, pf)
    x_da.relay()
    x_da.near()
    forward(da, mine, wa, 3 * QKV, QKV, put(datt, mine))
    y_ffn.give(0)
    y_ffn.give(1)
    y_ffn.give(2)
    y_ffn.give(3)
    x_da.far()
    forward(da, other, wa, 3 * QKV, QKV, put(datt, other))
    y_ffn.out()
    rsc("s00", "s10")
    heads(attend_back)
    gradient(a1, packed, ga, 0, 3 * QKV)
    rsc("f20", "f30")
    gradient(da, att, ga, 3 * QKV, QKV)
    rsc("f21", "f31")
    y_ffn.relay()
    rsc("r20", "r30")
    share(y_first, packed, 0, 3 * QKV)
    rsc("r21", "r31")
    rsc("e0", "e1")
    y_ffn.wait()
    by_rows(last_out)
    rsc("d2", "g2")
    y_first.wait()
    by_rows(first_back)
    rsc("d3", "g3", "s2", "s3", "e2", "e3")
    for h, out in enumerate((oi, ob)):
        arrive(out.at[:, pl.ds(other_f, HALF)], yr.at[h], me.across())
    sends.close()
    y_first.sends.close()
    y_ffn.sends.close()


def copy_kernel(*refs):
    n = len(refs) // 2
    sem = refs[-1]
    copies = [pltpu.make_async_copy(refs[i], refs[n + i], sem.at[i]) for i in range(n)]
    for copy in copies:
        copy.start()
    for copy in copies:
        copy.wait()


def copy_out(arrays):
    return pl.pallas_call(
        copy_kernel,
        out_shape=[jax.ShapeDtypeStruct(a.shape, a.dtype) for a in arrays],
        in_specs=[VM] * len(arrays),
        out_specs=[ANY] * len(arrays),
        scratch_shapes=[DMA((len(arrays),))],
    )(*arrays)


def local(tokens, modulation, w_qkv, w_out, w_in, w_back, out_grad):
    grad_scale = 1.0 / math.sqrt(OWN * lax.axis_size("sp") * lax.axis_size("fsdp"))
    factor = TEMPER / math.sqrt(HEAD_DIM)

    def shape(dims, dtype=BF16):
        return jax.ShapeDtypeStruct(dims, dtype)

    def vm(*dims, dtype=BF16):
        return pltpu.VMEM(dims, dtype)

    seq, ring = (4, OWN, WIDTH), (8, OWN, WIDTH)
    results = pl.pallas_call(
        functools.partial(step_kernel, grad_scale, factor),
        out_shape=(
            shape((OWN, WIDTH)), shape((OWN, WIDTH), F32), shape((3, ROWS, QKV), F32),
            shape((ROWS, QKV), F32), shape((ROWS, GROUP), F32), shape((ROWS, GROUP), F32),
        ),
        in_specs=[VM, VM, ANY, ANY, ANY, ANY, VM],
        out_specs=(VM,) * 6,
        scratch_shapes=[
            vm(4, 4, 2, ROWS, GROUP), vm(4, 4, 2, ROWS, GROUP), vm(4, 4, 2, ROWS, GROUP), vm(4, 4, 2, ROWS, GROUP),
            vm(4, 2, 2, 4, ROWS, QUART), vm(4, 2, 2, 4, ROWS, HALF),
            vm(4, 2, 2, ROWS, QUART), vm(4, 2, 2, ROWS, HALF),
            vm(2, ROWS, HALF), vm(2, ROWS, HALF), vm(2, ROWS, HALF, dtype=F32),
            vm(*seq), vm(*ring), vm(*ring), vm(*seq),
            vm(4, OWN, 3 * QKV), vm(4, OWN, QKV), vm(4, OWN, QKV),
            vm(8, OWN, HALF), vm(8, OWN, HALF, dtype=F32), vm(8, OWN, HALF),
            vm(*seq), vm(*ring), vm(2, OWN, WIDTH), vm(OWN, WIDTH), vm(OWN, WIDTH),
            vm(4, OWN, WIDTH), vm(2, 2, OWN, HALF), vm(2, 2, OWN, WIDTH), vm(OWN, WIDTH, dtype=F32),
            DMA((8, 8)), DMA((8, 8)), DMA((8, 8)), DMA((8, 8)),
            DMA((3,)), DMA((3,)), DMA((4,)), DMA((4,)), DMA((8, 9)), DMA((8, 9)), DMA((6,)),
        ],
        compiler_params=pltpu.CompilerParams(
            collective_id=0, has_side_effects=True, vmem_limit_bytes=67043328
        ),
    )(
        tokens[0], modulation.transpose(2, 0, 1, 3)[:, 0],
        w_qkv[0].transpose(1, 0, 2), w_out[0].T, w_in[0], w_back[0].T, out_grad[0],
    )
    final, grad, oq, oo, oi, ob = copy_out(results)
    return (
        final[None], grad[None], oq.transpose(1, 0, 2)[None], oo.T[None], oi[None], ob.T[None],
    )


def solution(mesh):
    weights = (
        P(None, "fsdp", None, "sp"),
        P(None, "sp", "fsdp"),
        P(None, "fsdp", "sp"),
        P(None, "sp", "fsdp"),
    )
    rows = P("fsdp", "sp", None)
    return jax.shard_map(
        local,
        mesh=mesh,
        in_specs=(rows, P("fsdp", None, None, None), *weights, rows),
        out_specs=(rows, rows, *weights),
        check_vma=False,
    )
```

time: 195 us -> 184 us (0.944)
  local copies, waits for them, and re-layouts: 9.58 us -> 0 us
    unnamed x25 -> x0, local copies, waits for them, and re-layouts: 9.58 us -> none
    pallas_call x0 -> x1, Pallas kernels: none -> 2.85 us  [copy_out(): pl.pallas_call(copy_kernel, out_shape=[jax.ShapeDtypeStruct(a.shape, a.dt...]
    pallas_call x1, Pallas kernels: 181 us -> 179 us  [local(): pl.pallas_call(functools.partial(step_kernel, grad_scale, factor), out_sh...]
where the time goes in v2:
time: 184 us; the launch traced here: 182 us
  Pallas kernels  182 us (99%)
    pallas_call x1, Pallas kernels, local(): pl.pallas_call(functools.partial(step_kernel, grad_scale, factor), out_sh...  179 us

profile of v2, /device:TPU:1, one launch (start us, length us, event | category | flops | bytes accessed | tf_op | source)
XLA Modules:
  0.0 182.4 jit_solution(5384696632488992031)
XLA Ops:
  0.6 178.8 %shard_map.118 = (bf16[128,1536]{1,0:T(8,128)(2,1)}, f32[128,1536]{1,0:T(8,128)}, f32[3,48,384]{2,1,0:T(8,128)}, f32[48,384]{1,0:T(8,128)}, f32[48,1536]{1,0:T(8,128)}, /*index=5*/f32[48,1536]{1,0:T(8,128)}) custom-call(bf16[128,1536]{1,0:T(8,128)(2,1)} %bitcast.25, f32[6,1,1536]{2,1,0:T(1,128)} %bitcast.30, bf16[3,48,384]{2,1,0:T(8,128)(2,1)} %bitcast.29, ...), custom_call_target="tpu_custom_call" | custom-call | tf_op jit(solution)/shard_map/pallas_call | solution.py:736
  179.4 2.8 %shard_map.119 = (bf16[128,1536]{1,0:T(8,128)(2,1)}, f32[128,1536]{1,0:T(8,128)}, f32[3,48,384]{2,1,0:T(8,128)}, f32[48,384]{1,0:T(8,128)}, f32[48,1536]{1,0:T(8,128)}, /*index=5*/f32[48,1536]{1,0:T(8,128)}) custom-call(bf16[128,1536]{1,0:T(8,128)(2,1)} %get-tuple-element.18.refs_0_, f32[128,1536]{1,0:T(8,128)} %get-tuple-element.19.refs_1_, ...), custom_call_target="tpu_custom_call" | custom-call | tf_op jit(solution)/shard_map/pallas_call | solution.py:716

commit v3 on v2

v3 whole, which is shorter than its diff:
```python
import functools
import math

import jax
import jax.numpy as jnp
from jax import lax
from jax.experimental import pallas as pl
from jax.experimental.pallas import tpu as pltpu
from jax.sharding import PartitionSpec as P

HEAD_DIM = 128
LN_EPS = 1e-06
TEMPER = 2.5
F32 = jnp.float32
BF16 = jnp.bfloat16
MESH = pl.DeviceIdType.MESH
GROUP = 1536
HALF = GROUP // 2
QUART = GROUP // 4
ROWS = 48


def rem(a, n):
    return lax.rem(a, n)


class Place:
    def __init__(self):
        f = lax.axis_index("fsdp")
        s = lax.axis_index("sp")
        self.z, self.y, self.xh = lax.div(f, 8), rem(lax.div(f, 2), 4), rem(f, 2)
        self.xl, self.c = lax.div(s, 2), rem(s, 2)
        self.s = s
        self.x = self.xh * 2 + self.xl
        self.n = self.x * 2 + self.c

    def dev(self, **kw):
        v = {k: kw.get(k, getattr(self, k)) for k in ("z", "y", "xh", "xl", "c")}
        return (v["z"] * 8 + v["y"] * 2 + v["xh"], v["xl"] * 2 + v["c"])

    def ring(self, axis, step):
        return rem(getattr(self, axis) + step + 4, 4)

    def near(self, axis, step):
        return self.dev(**{axis: self.ring(axis, step)})

    def along(self, step):
        x = rem(self.x + step + 4, 4)
        return self.dev(xh=lax.div(x, 2), xl=rem(x, 2))

    def chip_at(self, step):
        return rem(self.x + step + 4, 4)

    def across(self):
        return self.dev(xh=1 - self.xh)

    def chip(self):
        return self.dev(xl=1 - self.xl)

    def core(self):
        return self.dev(c=1 - self.c)


def greet(devices):
    barrier = pltpu.get_barrier_semaphore()
    for d in devices:
        pl.semaphore_signal(barrier, inc=1, device_id=d, device_id_type=MESH)
    pl.semaphore_wait(barrier, len(devices))


def torus_peers(me):
    return [me.near(a, s) for a in ("z", "y") for s in (1, -1)] + [me.across(), me.along(1), me.along(-1), me.core()]


class Sends:
    def __init__(self):
        self.open = []

    def start(self, src, dst, ssem, rsem, dev):
        copy = pltpu.make_async_remote_copy(
            src_ref=src, dst_ref=dst, send_sem=ssem, recv_sem=rsem, device_id=dev, device_id_type=MESH
        )
        copy.start()
        self.open.append(copy)

    def close(self):
        for copy in self.open:
            copy.wait_send()
        self.open = []


def arrive(ref, rsem, dev):
    pltpu.make_async_remote_copy(
        src_ref=ref, dst_ref=ref, send_sem=rsem, recv_sem=rsem, device_id=dev, device_id_type=MESH
    ).wait_recv()


def columns(start, low, high):
    return {"all": pl.ds(start, low + high), "lo": pl.ds(start, low), "hi": pl.ds(start + low, high)}


class Gather:
    def __init__(self, me, w, axes, span, xb, ssem, rsem, sends):
        self.me, self.w, self.axes, self.xb = me, w, axes, xb
        self.ssem, self.rsem, self.sends = ssem, rsem, sends
        self.cols = columns(*span)

    def part(self, p, q, which):
        first, second = self.axes
        at = {first: slice(None) if p is None else self.me.ring(first, p), second: self.me.ring(second, q)}
        return self.w.at[at["z"], at["y"], self.xb, :, self.cols[which]]

    def go(self, level, to, p, q, which, i):
        ref = self.part(p, q, which)
        self.sends.start(ref, ref, self.ssem.at[i], self.rsem.at[i], self.me.near(self.axes[level], to))

    def got(self, p, q, which, i):
        arrive(self.part(p, q, which), self.rsem.at[i], self.me.near(self.axes[0], 1))

    def first(self):
        self.go(0, 1, 0, 0, "all", 0)
        self.go(0, -1, 0, 0, "all", 1)

    def second(self):
        self.got(-1, 0, "all", 0)
        self.go(0, 1, -1, 0, "lo", 2)
        self.got(1, 0, "all", 1)
        self.go(0, -1, 1, 0, "hi", 3)

    def last(self):
        self.got(2, 0, "lo", 2)
        self.got(2, 0, "hi", 3)

    def out(self, *ps):
        for p in ps:
            i = 4 + (p + 1) * 2
            self.go(1, 1, p, 0, "all", i)
            self.go(1, -1, p, 0, "all", i + 1)

    def own(self):
        self.out(0)

    def sides(self):
        self.out(-1, 1)

    def end(self):
        self.out(2)

    def relay(self):
        for p in (0, -1, 1, 2):
            self.got(p, -1, "all", 4 + (p + 1) * 2)
        self.go(1, 1, None, -1, "lo", 12)
        for p in (0, -1, 1, 2):
            self.got(p, 1, "all", 5 + (p + 1) * 2)
        self.go(1, -1, None, 1, "hi", 13)

    def close(self):
        self.got(None, 2, "lo", 12)
        self.got(None, 2, "hi", 13)


def wider(ref_value):
    return ref_value.astype(F32)


def pack(total):
    return total.astype(BF16)


class Scatter:
    def __init__(self, me, g, axes, span, xb, bufs, ssem, rsem, sends):
        self.me, self.g, self.axes, self.xb = me, g, axes, xb
        self.bufs, self.ssem, self.rsem, self.sends = bufs, ssem, rsem, sends
        self.cols = columns(*span)
        self.inner = columns(0, *span[1:])

    def spot(self, level, step, which):
        axis = self.axes[level]
        at = {"z": self.me.z, "y": self.me.y}
        at[axis] = self.me.ring(axis, step)
        if level == 0:
            at[self.axes[1]] = slice(None)
        return (at["z"], at["y"], self.xb, slice(None), self.cols[which])

    def way(self, level, i, which):
        if level == 0:
            return self.bufs[0][0].at[i, :, :, columns(0, *self.sizes(which))["lo"]]
        return self.bufs[1][0].at[i, :, columns(0, *self.sizes(which))["lo"]]

    def sizes(self, which):
        return self.inner[which].size, 0

    def send(self, level, step, which, dst, i, to):
        i = level * 6 + i
        self.sends.start(
            self.g.at[self.spot(level, step, which)], dst, self.ssem.at[i], self.rsem.at[i],
            self.me.near(self.axes[level], to),
        )

    def near(self, level, i, which):
        cols = self.inner[which]
        if level == 0:
            return self.bufs[level][1].at[i, :, :, cols]
        return self.bufs[level][1].at[i, :, cols]

    def far(self, level):
        for to, which, i in ((1, "lo", 0), (-1, "hi", 1)):
            self.send(level, 2, which, self.way(level, i, which), i, to)

    def rest(self, level):
        for to, which, i in ((1, "hi", 0), (-1, "lo", 1)):
            self.send(level, to, which, self.near(level, i, which), 4 + i, to)

    def both(self, level):
        self.far(level)
        self.rest(level)

    def relay(self, level):
        for to, which, i in ((1, "lo", 0), (-1, "hi", 1)):
            buf = self.way(level, i, which)
            arrive(buf, self.rsem.at[level * 6 + i], self.me.near(self.axes[level], -to))
            spot = self.spot(level, to, which)
            self.g[spot] = (wider(self.g[spot]) + wider(buf[...])).astype(BF16)
        for to, which, i in ((1, "lo", 0), (-1, "hi", 1)):
            self.send(level, to, which, self.near(level, i, which), 2 + i, to)

    def total(self, level):
        near = self.bufs[level][1]
        for which, i, j in (("hi", 0, 4), ("lo", 1, 5), ("lo", 0, 2), ("hi", 1, 3)):
            arrive(self.near(level, i, which), self.rsem.at[level * 6 + j], self.me.near(self.axes[level], 1))
        spot = self.spot(level, 0, "all")
        return spot, wider(self.g[spot]) + wider(near[0]) + wider(near[1])

    def fold(self):
        spot, total = self.total(0)
        self.g[spot] = total.astype(BF16)


class FineScatter(Scatter):
    slots = {2: 0, 1: 1, -1: 2, 0: 3}
    lines = (0, 12, 18, 24)

    def place(self, q, p, which):
        at = {self.axes[0]: self.me.ring(self.axes[0], q), self.axes[1]: self.me.ring(self.axes[1], p)}
        return (at["z"], at["y"], self.xb, slice(None), self.cols[which])

    def give(self, q, p, which, dst, i, to):
        i = self.lines[self.slots[p]] + i
        self.sends.start(
            self.g.at[self.place(q, p, which)], dst, self.ssem.at[i], self.rsem.at[i], self.me.near(self.axes[0], to)
        )

    def take(self, dst, p, i):
        arrive(dst, self.rsem.at[self.lines[self.slots[p]] + i], self.me.near(self.axes[0], 1))

    def side(self, i, p, which):
        return self.bufs[0][1].at[i, self.slots[p], :, self.inner[which]]

    def step(self, i, p, which):
        return self.bufs[0][0].at[i, self.slots[p], :, pl.ds(0, self.inner[which].size)]

    def far0(self, *ps):
        for p in ps:
            for to, which, i in ((1, "lo", 0), (-1, "hi", 1)):
                self.give(2, p, which, self.step(i, p, which), i, to)

    def rest0(self, *ps):
        for p in ps:
            for to, which, i in ((1, "hi", 0), (-1, "lo", 1)):
                self.give(to, p, which, self.side(i, p, which), 4 + i, to)

    def relay0(self, *ps):
        for p in ps:
            for to, which, i in ((1, "lo", 0), (-1, "hi", 1)):
                buf = self.step(i, p, which)
                self.take(buf, p, i)
                spot = self.place(to, p, which)
                self.g[spot] = pack(wider(self.g[spot]) + wider(buf[...]))
            for to, which, i in ((1, "lo", 0), (-1, "hi", 1)):
                self.give(to, p, which, self.side(i, p, which), 2 + i, to)

    def fold0(self, *ps):
        for p in ps:
            for which, i, j in (("hi", 0, 4), ("lo", 1, 5), ("lo", 0, 2), ("hi", 1, 3)):
                self.take(self.side(i, p, which), p, j)
            spot = self.place(0, p, "all")
            near = self.bufs[0][1]
            total = wider(self.g[spot]) + wider(near[0, self.slots[p]]) + wider(near[1, self.slots[p]])
            self.g[spot] = pack(total)


DMA = pltpu.SemaphoreType.DMA
VM = pl.BlockSpec(memory_space=pltpu.VMEM)
ANY = pl.BlockSpec(memory_space=pl.ANY)
OWN = 128
WIDTH = 1536
HEADS = 3
QKV = HEADS * HEAD_DIM
GELU_A = math.sqrt(2.0 / math.pi)
GELU_B = 0.044715


CHUNKS = ((0, OWN // 2), (OWN // 2, OWN // 2))


class SeqGather:
    def __init__(self, me, buf, rows, ssem, rsem, sends):
        self.me, self.buf, self.rows, self.ssem, self.rsem, self.sends = me, buf, pl.ds(*rows), ssem, rsem, sends

    def push(self, block, i, dev):
        ref = self.buf.at[block, self.rows]
        self.sends.start(ref, ref, self.ssem.at[i], self.rsem.at[i], dev)

    def start(self):
        self.push(self.me.s, 0, self.me.chip())
        self.push(self.me.s, 1, self.me.core())

    def relay(self):
        other = (1 - self.me.xl) * 2 + self.me.c
        arrive(self.buf.at[other, self.rows], self.rsem.at[0], self.me.chip())
        self.push(other, 2, self.me.core())

    def near(self):
        arrive(self.buf.at[self.me.xl * 2 + 1 - self.me.c, self.rows], self.rsem.at[1], self.me.core())

    def far(self):
        arrive(self.buf.at[(1 - self.me.xl) * 2 + 1 - self.me.c, self.rows], self.rsem.at[2], self.me.core())


class SeqScatter:
    def __init__(self, me, part, swap, mine, theirs, ssem, rsem):
        self.me, self.part, self.swap, self.mine, self.theirs = me, part, swap, mine, theirs
        self.ssem, self.rsem, self.sends = ssem, rsem, Sends()

    def give(self, i):
        xl = self.me.xl if i else 1 - self.me.xl
        self.sends.start(
            self.part.at[xl * 2 + 1 - self.me.c], self.swap.at[i], self.ssem.at[i], self.rsem.at[i], self.me.core()
        )

    def cross(self):
        arrive(self.swap.at[0], self.rsem.at[0], self.me.core())

        def merge(r):
            self.mine[r] = pack(wider(self.part[(1 - self.me.xl) * 2 + self.me.c, r]) + wider(self.swap[0, r]))

        for i, rows in enumerate(CHUNKS):
            by_rows(merge, rows)
            r = pl.ds(*rows)
            self.sends.start(
                self.mine.at[r], self.theirs.at[r], self.ssem.at[2 + i], self.rsem.at[2 + i], self.me.chip()
            )

    def wait(self, i):
        if i == 0:
            arrive(self.swap.at[1], self.rsem.at[1], self.me.core())
        arrive(self.theirs.at[pl.ds(*CHUNKS[i])], self.rsem.at[2 + i], self.me.chip())

    def rows(self, r):
        return wider(self.part[self.me.s, r]) + wider(self.swap[1, r]) + wider(self.theirs[r])


LEFT, RIGHT = pl.ds(0, HALF), pl.ds(HALF, HALF)


class RingGather:
    def __init__(self, me, buf, rows, ssem, rsem, sends):
        self.me, self.buf, self.rows, self.ssem, self.rsem, self.sends = me, buf, pl.ds(*rows), ssem, rsem, sends

    def at(self, step, mine=True, cols=pl.ds(0, WIDTH)):
        return self.buf.at[self.me.chip_at(step) * 2 + (self.me.c if mine else 1 - self.me.c), self.rows, cols]

    def push(self, ref, i, dev):
        self.sends.start(ref, ref, self.ssem.at[i], self.rsem.at[i], dev)

    def start(self):
        for cols, step, i in ((LEFT, 1, 0), (RIGHT, -1, 1), (RIGHT, 1, 9), (LEFT, -1, 10)):
            self.push(self.at(0, cols=cols), i, self.me.along(step))
        self.push(self.at(0), 2, self.me.core())

    def relay(self):
        for step, cols, i in ((-1, LEFT, 0), (1, RIGHT, 1)):
            arrive(self.at(step, cols=cols), self.rsem.at[i], self.me.core())
            self.push(self.at(step, cols=cols), 3 + i, self.me.along(-step))

    def spread(self):
        for step, cols, i in ((-1, RIGHT, 0), (1, LEFT, 1)):
            arrive(self.at(step, cols=cols), self.rsem.at[9 + i], self.me.core())
            self.push(self.at(step), 5 + i, self.me.core())

    def last(self):
        for cols, i in ((LEFT, 0), (RIGHT, 1)):
            arrive(self.at(2, cols=cols), self.rsem.at[3 + i], self.me.core())
            self.push(self.at(2, cols=cols), 7 + i, self.me.core())

    def own(self):
        arrive(self.at(0, False), self.rsem.at[2], self.me.core())

    def sides(self):
        for step, i in ((-1, 5), (1, 6)):
            arrive(self.at(step, False), self.rsem.at[i], self.me.core())

    def far(self):
        for cols, i in ((LEFT, 7), (RIGHT, 8)):
            arrive(self.at(2, False, cols), self.rsem.at[i], self.me.core())


class RingScatter:
    order = (2, 1, -1, 0)

    def __init__(self, me, part, swap, away, near, rows, ssem, rsem):
        self.me, self.part, self.swap, self.away, self.near = me, part, swap, away, near
        self.span, self.ssem, self.rsem, self.sends = rows, ssem, rsem, Sends()
        self.r = pl.ds(*rows)

    def block(self, step):
        return self.me.chip_at(step) * 2 + self.me.c

    def give(self, j):
        src = self.part.at[self.me.chip_at(self.order[j]) * 2 + 1 - self.me.c]
        self.sends.start(src, self.swap.at[j], self.ssem.at[j], self.rsem.at[j], self.me.core())

    def swapped(self, j):
        if self.span[0] == 0:
            arrive(self.swap.at[j], self.rsem.at[j], self.me.core())

    def push(self, step, cols, dst, i, to):
        self.sends.start(
            self.part.at[self.block(step), self.r, cols], dst, self.ssem.at[i], self.rsem.at[i], self.me.along(to)
        )

    def out(self):
        self.swapped(0)
        block = self.block(2)

        def merge(r):
            self.part[block, r] = pack(wider(self.part[block, r]) + wider(self.swap[0, r]))

        by_rows(merge, self.span)
        self.push(2, LEFT, self.away.at[0, self.r], 4, 1)
        self.push(2, RIGHT, self.away.at[1, self.r], 5, -1)

    def rest(self):
        for step, j, i, cols in ((1, 1, 0, RIGHT), (-1, 2, 1, LEFT)):
            self.swapped(j)
            block = self.block(step)

            def merge(r):
                self.part[block, r, cols] = pack(wider(self.part[block, r, cols]) + wider(self.swap[j, r, cols]))

            by_rows(merge, self.span)
            self.push(step, cols, self.near.at[i, self.r, cols], 8 + i, step)

    def relay(self):
        for step, j, i, cols in ((1, 1, 0, LEFT), (-1, 2, 1, RIGHT)):
            arrive(self.away.at[i, self.r], self.rsem.at[4 + i], self.me.core())
            block = self.block(step)

            def merge(r):
                both = wider(self.part[block, r, cols]) + wider(self.swap[j, r, cols])
                self.part[block, r, cols] = pack(both + wider(self.away[i, r]))

            by_rows(merge, self.span)
            self.push(step, cols, self.near.at[i, self.r, cols], 6 + i, step)

    def wait(self):
        self.swapped(3)
        for i, cols, rest in ((0, LEFT, RIGHT), (1, RIGHT, LEFT)):
            arrive(self.near.at[i, self.r, rest], self.rsem.at[8 + i], self.me.core())
            arrive(self.near.at[i, self.r, cols], self.rsem.at[6 + i], self.me.core())

    def rows(self, r):
        own = wider(self.part[self.block(0), r]) + wider(self.swap[3, r])
        return own + (wider(self.near[0, r]) + wider(self.near[1, r]))


def normalize(stream):
    centred = stream - jnp.mean(stream, axis=-1, keepdims=True)
    rstd = lax.rsqrt(jnp.mean(centred * centred, axis=-1, keepdims=True) + LN_EPS)
    return (centred * rstd, rstd)


def norm_back(normed, rstd, incoming):
    first = jnp.mean(incoming, axis=-1, keepdims=True)
    second = jnp.mean(incoming * normed, axis=-1, keepdims=True)
    return rstd * (incoming - first - normed * second)


def contract(left, right, left_dim, right_dim):
    return lax.dot_general(
        left, right, (((left_dim,), (right_dim,)), ((), ())), preferred_element_type=F32
    )


def softmax_rows(queries, key_rows, factor):
    scores = contract(queries, key_rows, 1, 1) * factor
    scores = jnp.exp(scores - jnp.max(scores, axis=-1, keepdims=True))
    return scores * (1.0 / jnp.sum(scores, axis=-1, keepdims=True))


def by_rows(body, rows=(0, OWN)):
    @pl.loop(rows[0] // 32, (rows[0] + rows[1]) // 32)
    def _(i):
        body(pl.ds(pl.multiple_of(i * 32, 32), 32))


def step_kernel(
    grad_scale, factor,
    tok, mod, wq, wo, wi, wb, og,
    final, grad, oq, oo, oi, ob,
    wa, wf, ga, gf, r1, r2, p1, p2, r3, r4, p3, p4, xbuf, part, partf, xf, a1, a2, dm, da, packed, att, datt, act, dg, du,
    pf, swap, own_sum, theirs, swapf, away, near, middle,
    gs, gr, ss, rs, xs, xr, ys, yr, es, er, csem,
):
    me = Place()
    mine_f = pl.multiple_of(me.xh * HALF, HALF)
    other_f = pl.multiple_of((1 - me.xh) * HALF, HALF)
    home_a, home_f = wa.at[me.z, me.y, me.xh], wf.at[me.z, me.y, me.xh]
    parts = [
        (wq.at[j, :, pl.ds(h * HEAD_DIM, HEAD_DIM)], home_a.at[:, pl.ds(h * QKV + j * HEAD_DIM, HEAD_DIM)])
        for h in range(HEADS) for j in range(3)
    ] + [
        (wo, home_a.at[:, pl.ds(3 * QKV, QKV)]),
        (wi.at[:, pl.ds(mine_f, HALF)], home_f.at[:, LEFT]),
        (wb.at[:, pl.ds(mine_f, HALF)], home_f.at[:, RIGHT]),
    ]
    loads = [pltpu.make_async_copy(src, dst, csem.at[i]) for i, (src, dst) in enumerate(parts)]
    for load in loads:
        load.start()
    greet(torus_peers(me))
    for load in loads:
        load.wait()
    mine, other = me.xl, 1 - me.xl

    def m(i):
        return mod[i]

    sends = Sends()
    yz, zy = ("y", "z"), ("z", "y")
    plan = [
        (wa, 0, [(yz, (0, 384, 256)), (zy, (640, 256, 256))]), (wa, 1, [(zy, (0, 384, 256)), (yz, (640, 256, 256))]),
        (wa, 0, [(yz, (1152, 256, 128))]), (wa, 1, [(zy, (1152, 256, 128))]),
        (wf, 0, [(yz, (0, 384, 384)), (zy, (768, 384, 384))]), (wf, 1, [(yz, (0, 384, 384)), (zy, (768, 384, 384))]),
    ]
    pieces = []
    count = 0
    for ref, side, halves in plan:
        pieces.append([])
        for axes, span in halves:
            xb = 1 - me.xh if side else me.xh
            pieces[-1].append(Gather(me, ref, axes, span, xb, gs.at[count], gr.at[count], sends))
            count += 1

    def gather_event(k, what):
        if what == "first" and k % 2:
            for i, ref, cols in crossed[k]:
                arrive(ref.at[me.z, me.y, 1 - me.xh, :, cols], xr.at[i], me.across())
        for half in pieces[k]:
            getattr(half, what)()

    crossed = {1: [(0, wa, pl.ds(0, 3 * QKV))], 3: [(1, wa, pl.ds(3 * QKV, QKV))], 5: [(2, wf, LEFT), (3, wf, RIGHT)]}

    def cross(group):
        if group < 2:
            ref = home_a.at[:, crossed[2 * group + 1][0][2]]
            sends.start(ref, ref, xs.at[group], xr.at[group], me.across())
        else:
            for i, ref, cols in ((2, wi, LEFT), (3, wb, RIGHT)):
                sends.start(ref.at[:, pl.ds(other_f, HALF)], home_f.at[:, cols], xs.at[i], xr.at[i], me.across())

    def ag(*steps):
        names = {
            "f": "first", "s": "second", "l": "last", "o": "own", "i": "sides", "e": "end", "r": "relay", "c": "close"
        }
        for step in steps:
            gather_event(int(step[1]), names[step[0]])

    scatters = []
    for k in range(10):
        side = k % 2
        xb = me.xh if side else 1 - me.xh
        if k < 4:
            span, axes = ((HALF, 384, 384), (0, 384, 384))[k // 2], (yz, zy, zy, yz)[k]
        else:
            span, axes = ((3 * QKV, 256, 128), (0, 384, 384), (2 * QKV, 256, 128))[k // 2 - 2], (zy, yz, zy, yz, yz, zy)[k - 4]
        kind = Scatter if k < 4 else FineScatter
        if span[1] == 384:
            n = k if k < 4 else k - 2
            bufs = ((r1.at[n], r2.at[n]), (p1.at[n], p2.at[n]))
        else:
            n = k - 4 if k < 6 else k - 6
            bufs = ((r3.at[n], r4.at[n]), (p3.at[n], p4.at[n]))
        scatters.append(kind(me, gf if k < 4 else ga, axes, span, xb, bufs, ss.at[k], rs.at[k], sends))

    def finish(k):
        scatter = scatters[k]
        _, total = scatter.total(1)
        cols = scatter.cols["all"]
        group = k // 2
        if k < 4:
            out = (ob, oi)[group].at[:, pl.ds(mine_f, HALF)]
            if k % 2:
                out[...] = total
            else:
                partf[group] = pack(total)
                sends.start(partf.at[group], xf.at[group], ys.at[group], yr.at[group], me.across())
        elif k % 2 == 0:
            part[:, cols] = pack(total)
            sends.start(part.at[:, cols], xbuf.at[:, cols], ys.at[group], yr.at[group], me.across())
        else:
            arrive(xbuf.at[:, cols], yr.at[group], me.across())
            total = total + wider(xbuf[:, cols])
            for i in range(cols.size // QKV):
                value = total[:, i * QKV : (i + 1) * QKV]
                head = cols.start // QKV + i
                if head == HEADS:
                    oo[...] = value
                else:
                    for j in range(3):
                        oq[j, :, pl.ds(head * HEAD_DIM, HEAD_DIM)] = value[:, j * HEAD_DIM : (j + 1) * HEAD_DIM]

    def rsc(*steps):
        names = {
            "f": ("both", 0), "r": ("relay", 0), "d": ("fold",), "g": ("both", 1), "s": ("relay", 1),
            "F": ("far0",), "N": ("rest0",), "R": ("relay0",), "D": ("fold0",), "G": ("far", 1), "H": ("rest", 1),
        }
        spots = {"": (2, 1, -1, 0), "a": (2,), "b": (1, -1), "c": (0,), "ab": (2, 1, -1), "bc": (1, -1, 0)}
        for step in steps:
            scatter_event(step, int(step[1]), names, spots)

    def scatter_event(step, k, names, spots):
        if step[0] == "e":
            finish(k)
        else:
            name, *args = names[step[0]]
            if step[0] in "FNRD":
                args = spots[step[2:]]
            getattr(scatters[k], name)(*args)

    def rows_of(ref, side, cols=slice(None)):
        value = ref[pl.ds(side * 2, 2), :, cols]
        return value.reshape(2 * OWN, value.shape[-1])

    def forward(src, side, w, col, width, emit):
        weight = w[:, :, :, :, pl.ds(col, width)].reshape(WIDTH, width)
        emit(contract(rows_of(src, side), weight, 1, 0).reshape(2, OWN, width))

    def backward(src, side, w, col, width, out):
        @pl.loop(0, 2)
        def _(j):
            weight = w[pl.ds(j * 2, 2), :, :, :, pl.ds(col, width)].reshape(HALF, width)
            at = pl.multiple_of(j * HALF, 128)
            value = contract(rows_of(src, side), weight, 1, 1)
            out[pl.ds(side * 2, 2), :, pl.ds(at, HALF)] = pack(value).reshape(2, OWN, HALF)

    def gradient(left, right, g, col, width):
        count = left.shape[0] * OWN

        @pl.loop(0, 4)
        def _(j):
            rows = left[:, :, pl.ds(pl.multiple_of(j * 384, 128), 384)].reshape(count, 384)
            value = contract(rows, right[...].reshape(count, width), 0, 0) * grad_scale
            g[j, :, :, :, pl.ds(col, width)] = pack(value).reshape(4, 2, ROWS, width)

    every = (0, OWN)
    x_a1 = SeqGather(me, a1, every, es.at[0], er.at[0], sends)
    x_das = [SeqGather(me, da, rows, es.at[1 + i], er.at[1 + i], sends) for i, rows in enumerate(CHUNKS)]
    a2_sends = Sends()
    x_a2s = [RingGather(me, a2, rows, es.at[3 + i], er.at[3 + i], a2_sends) for i, rows in enumerate(CHUNKS)]
    x_dm = RingGather(me, dm, every, es.at[5], er.at[5], sends)
    y_att = SeqScatter(me, pf.at[pl.ds(0, 4)], swap, own_sum, theirs, es.at[6], er.at[6])
    y_first = SeqScatter(me, a2.at[pl.ds(0, 4)], swap, own_sum, theirs, es.at[7], er.at[7])
    y_backs = [
        RingScatter(me, pf, swapf.at[0], away.at[0], near.at[0], rows, es.at[8 + i], er.at[8 + i])
        for i, rows in enumerate(CHUNKS)
    ]
    y_back = y_backs[0]
    y_ffn = RingScatter(me, pf, swapf.at[1], away.at[1], near.at[1], every, es.at[10], er.at[10])

    def all_of(objects, *names):
        for name in names:
            for item in objects:
                getattr(item, name)()

    def share(y, src, col, width):
        backward(src, other, wa, col, width, y.part)
        y.give(0)
        backward(src, mine, wa, col, width, y.part)
        y.give(1)
        y.cross()

    def first_norm(r):
        n1, _ = normalize(wider(tok[r]))
        a1[me.s, r] = pack(n1 * (1.0 + m(1)) + m(0))

    def gate(r):
        dm[me.n, r] = pack(m(5) * wider(og[r]))

    def put(dst, side):
        def emit(value):
            dst[pl.ds(side * 2, 2)] = pack(value)
        return emit

    def head_cols(place, head):
        return pl.ds(pl.multiple_of(head * QKV + place * HEAD_DIM, HEAD_DIM), HEAD_DIM)

    def own_cols(head):
        return pl.ds(pl.multiple_of(head * HEAD_DIM, HEAD_DIM), HEAD_DIM)

    def head_rows(ref, cols):
        return ref[:, :, cols].reshape(4 * OWN, HEAD_DIM)

    def attend(head):
        q, k, v = (head_rows(packed, head_cols(i, head)) for i in range(3))
        probs = softmax_rows(q, k, factor)
        att[:, :, own_cols(head)] = pack(contract(pack(probs), v, 1, 0)).reshape(4, OWN, HEAD_DIM)

    def attend_back(head):
        q, k, v = (head_rows(packed, head_cols(i, head)) for i in range(3))
        up = head_rows(datt, own_cols(head))
        probs = softmax_rows(q, k, factor)
        dprobs = contract(up, v, 1, 1)
        dscores = pack(probs * (dprobs - jnp.sum(probs * dprobs, axis=-1, keepdims=True)) * factor)
        parts = (contract(dscores, k, 1, 0), contract(dscores, q, 0, 0), contract(pack(probs), up, 0, 0))
        for i, value in enumerate(parts):
            packed[:, :, head_cols(i, head)] = pack(value).reshape(4, OWN, HEAD_DIM)

    def heads(body, low=0, high=HEADS):
        pl.loop(low, high)(body)

    def second_norm(r):
        mid = wider(tok[r]) + m(2) * y_att.rows(r)
        middle[r] = mid
        n2, _ = normalize(mid)
        a2[me.n, r] = pack(n2 * (1.0 + m(4)) + m(3))

    def hidden(chip):
        def emit(u):
            t = jnp.tanh(GELU_A * (u + GELU_B * (u * u * u)))
            at = pl.ds(chip * 2, 2)
            act[at] = pack(0.5 * u * (1.0 + t))
            slope = 0.5 * (1.0 + t) + (0.5 * GELU_A) * u * (1.0 - t * t) * (1.0 + (3.0 * GELU_B) * (u * u))
            du[at] = pack(slope * dg[at])
        forward(a2, chip, wf, 0, HALF, emit)

    def hidden_back(chip):
        def emit(value):
            dg[pl.ds(chip * 2, 2)] = value
        forward(dm, chip, wf, HALF, HALF, emit)

    def middle_back(r):
        n2, rstd = normalize(middle[r])
        up = wider(og[r]) + norm_back(n2, rstd, y_back.rows(r) * (1.0 + m(4)))
        grad[r] = up
        da[me.s, r] = pack(m(2) * up)

    def last_out(r):
        final[r] = pack(middle[r] + m(5) * y_ffn.rows(r))

    def first_back(r):
        n1, rstd = normalize(wider(tok[r]))
        grad[r] = grad[r] + norm_back(n1, rstd, y_first.rows(r) * (1.0 + m(1)))

    def sides(i):
        hidden(me.chip_at(2 * i - 1))

    def backs(i):
        hidden_back(me.chip_at(i))

    def norm_and_send(i):
        y_att.wait(i)
        by_rows(second_norm, CHUNKS[i])
        x_a2s[i].start()

    def back_and_send(i):
        y_backs[i].wait()
        by_rows(middle_back, CHUNKS[i])
        x_das[i].start()

    def norm_and_send(i):
        y_att.wait(i)
        by_rows(second_norm, CHUNKS[i])
        x_a2s[i].start()

    def back_and_send(i):
        y_backs[i].wait()
        by_rows(middle_back, CHUNKS[i])
        x_das[i].start()

    cross(0)
    ag("f0", "o0", "f4", "o4")
    by_rows(first_norm)
    x_a1.start()
    cross(1)
    cross(2)
    by_rows(gate)
    x_dm.start()
    ag("s0", "i0", "f1", "o1", "l0", "e0", "f2", "s1", "i1", "l1", "e1", "r0", "s2", "f3")
    x_a1.relay()
    ag("o2", "i2", "l2", "r1", "e2", "o3", "s3", "i3")
    x_dm.relay()
    ag("l3", "e3", "c0")
    x_a1.near()
    x_a1.far()
    ag("c1")
    forward(a1, mine, wa, 0, 3 * QKV, put(packed, mine))
    forward(a1, other, wa, 0, 3 * QKV, put(packed, other))
    ag("s4", "r2")
    heads(attend, 0, 1)
    ag("r3", "i4", "f5")
    heads(attend, 1, 3)
    ag("c2", "c3")
    share(y_att, att, 3 * QKV, QKV)
    x_dm.spread()
    ag("l4", "e4", "s5", "o5", "i5", "l5", "e5")
    x_dm.last()
    x_dm.own()
    x_dm.sides()
    x_dm.far()
    ag("r4")
    norm_and_send(0)
    norm_and_send(1)
    ag("r5")
    x_a2s[0].relay()
    y_att.sends.close()
    all_of(x_a2s, "own")
    ag("c4", "c5")
    pl.loop(0, 2)(backs)
    x_a2s[1].relay()
    hidden(me.x)
    pl.loop(2, 4)(backs)
    all_of(x_a2s, "spread", "sides")
    pl.loop(0, 2)(sides)
    all_of(x_a2s, "last")

    backward(du, me.chip_at(1), wf, 0, HALF, pf)
    y_back.give(1)
    all_of(x_a2s, "far")
    hidden(me.chip_at(2))
    backward(du, me.chip_at(2), wf, 0, HALF, pf)
    y_back.give(0)
    backward(du, me.chip_at(-1), wf, 0, HALF, pf)
    y_back.give(2)
    all_of(y_backs, "out")
    backward(du, me.chip_at(0), wf, 0, HALF, pf)
    y_back.give(3)
    all_of(y_backs, "rest")
    gradient(dm, act, gf, HALF, HALF)
    rsc("f0", "f1")
    all_of(y_backs, "relay")
    gradient(a2, du, gf, 0, HALF)
    rsc("r0", "r1", "f2", "f3")
    back_and_send(0)
    back_and_send(1)
    y_backs[0].sends.close()
    y_backs[1].sends.close()
    a2_sends.close()
    backward(act, me.chip_at(2), wf, HALF, HALF, pf)
    y_ffn.give(0)
    backward(act, me.chip_at(1), wf, HALF, HALF, pf)
    y_ffn.give(1)
    rsc("d0", "g0", "d1", "g1")
    x_das[0].relay()
    backward(act, me.chip_at(-1), wf, HALF, HALF, pf)
    y_ffn.give(2)
    rsc("r2", "r3")
    backward(act, me.chip_at(0), wf, HALF, HALF, pf)
    y_ffn.give(3)
    x_das[1].relay()
    all_of(x_das, "near")
    forward(da, mine, wa, 3 * QKV, QKV, put(datt, mine))
    all_of(x_das, "far")
    forward(da, other, wa, 3 * QKV, QKV, put(datt, other))
    y_ffn.out()
    gradient(da, att, ga, 3 * QKV, QKV)
    rsc("F4", "F5", "N4", "N5")
    heads(attend_back, 0, 2)
    y_ffn.rest()
    rsc("d2", "g2", "d3", "g3", "s0", "s1")
    gradient(a1, packed.at[:, :, pl.ds(0, HALF)], ga, 0, HALF)
    rsc("F6", "F7", "N6", "N7", "R4", "R5")
    heads(attend_back, 2, 3)
    gradient(a1, packed.at[:, :, pl.ds(HALF, QKV)], ga, HALF, QKV)
    rsc("F8", "F9", "N8", "N9", "s2", "s3", "R6a", "R7a", "R6b", "R7b", "R6c", "R7c", "e0")
    y_ffn.relay()
    share(y_first, packed, 0, 3 * QKV)
    rsc("R8a", "R9a", "R8b", "R9b", "R8c", "R9c", "e2", "D4", "G4", "H4", "D5", "G5", "H5")
    rsc("D6a", "G6", "D7a", "G7", "D6b", "H6", "D7b", "H7", "D6c", "D7c")
    rsc("D8a", "G8", "D9a", "G9", "D8b", "H8", "D9b", "H9", "D8c", "D9c", "s4", "s5", "s6", "s7", "s8", "s9")
    rsc("e4", "e6", "e8")
    y_ffn.wait()
    by_rows(last_out)
    y_first.wait(0)
    y_first.wait(1)
    by_rows(first_back)
    rsc("e1", "e3")
    for group, out in enumerate((ob, oi)):
        arrive(xf.at[group], yr.at[group], me.across())
        out[:, pl.ds(other_f, HALF)] = wider(xf[group])
    rsc("e5", "e7", "e9")
    sends.close()
    y_first.sends.close()
    y_ffn.sends.close()


def copy_kernel(*refs):
    n = len(refs) // 2
    sem = refs[-1]
    copies = [pltpu.make_async_copy(refs[i], refs[n + i], sem.at[i]) for i in range(n)]
    for copy in copies:
        copy.start()
    for copy in copies:
        copy.wait()


def copy_out(arrays):
    return pl.pallas_call(
        copy_kernel,
        out_shape=[jax.ShapeDtypeStruct(a.shape, a.dtype) for a in arrays],
        in_specs=[VM] * len(arrays),
        out_specs=[ANY] * len(arrays),
        scratch_shapes=[DMA((len(arrays),))],
    )(*arrays)


def local(tokens, modulation, w_qkv, w_out, w_in, w_back, out_grad):
    grad_scale = 1.0 / math.sqrt(OWN * lax.axis_size("sp") * lax.axis_size("fsdp"))
    factor = TEMPER / math.sqrt(HEAD_DIM)

    def shape(dims, dtype=BF16):
        return jax.ShapeDtypeStruct(dims, dtype)

    def vm(*dims, dtype=BF16):
        return pltpu.VMEM(dims, dtype)

    seq, ring = (4, OWN, WIDTH), (8, OWN, WIDTH)
    results = pl.pallas_call(
        functools.partial(step_kernel, grad_scale, factor),
        out_shape=(
            shape((OWN, WIDTH)), shape((OWN, WIDTH), F32), shape((3, ROWS, QKV), F32),
            shape((ROWS, QKV), F32), shape((ROWS, GROUP), F32), shape((ROWS, GROUP), F32),
        ),
        in_specs=[VM, VM, ANY, ANY, ANY, ANY, VM],
        out_specs=(VM,) * 6,
        scratch_shapes=[
            vm(4, 4, 2, ROWS, GROUP), vm(4, 4, 2, ROWS, GROUP), vm(4, 4, 2, ROWS, GROUP), vm(4, 4, 2, ROWS, GROUP),
            vm(6, 2, 4, ROWS, QUART), vm(6, 2, 4, ROWS, HALF), vm(6, 2, ROWS, QUART), vm(6, 2, ROWS, HALF),
            vm(4, 2, 4, ROWS, 256), vm(4, 2, 4, ROWS, 384), vm(4, 2, ROWS, 256), vm(4, 2, ROWS, 384),
            vm(ROWS, GROUP), vm(ROWS, GROUP), vm(2, ROWS, HALF), vm(2, ROWS, HALF),
            vm(*seq), vm(*ring), vm(*ring), vm(*seq),
            vm(4, OWN, 3 * QKV), vm(4, OWN, QKV), vm(4, OWN, QKV),
            vm(8, OWN, HALF), vm(8, OWN, HALF, dtype=F32), vm(8, OWN, HALF),
            vm(*ring), vm(2, OWN, WIDTH), vm(OWN, WIDTH), vm(OWN, WIDTH),
            vm(2, 4, OWN, WIDTH), vm(2, 2, OWN, HALF), vm(2, 2, OWN, WIDTH), vm(OWN, WIDTH, dtype=F32),
            DMA((10, 14)), DMA((10, 14)), DMA((10, 30)), DMA((10, 30)),
            DMA((4,)), DMA((4,)), DMA((5,)), DMA((5,)), DMA((11, 11)), DMA((11, 11)), DMA((12,)),
        ],
        compiler_params=pltpu.CompilerParams(
            collective_id=0, has_side_effects=True, vmem_limit_bytes=67043328
        ),
    )(
        tokens[0], modulation.transpose(2, 0, 1, 3)[:, 0],
        w_qkv[0].transpose(1, 0, 2), w_out[0].T, w_in[0], w_back[0].T, out_grad[0],
    )
    final, grad, oq, oo, oi, ob = copy_out(results)
    return (
        final[None], grad[None], oq.transpose(1, 0, 2)[None], oo.T[None], oi[None], ob.T[None],
    )


def solution(mesh):
    weights = (
        P(None, "fsdp", None, "sp"),
        P(None, "sp", "fsdp"),
        P(None, "fsdp", "sp"),
        P(None, "sp", "fsdp"),
    )
    rows = P("fsdp", "sp", None)
    return jax.shard_map(
        local,
        mesh=mesh,
        in_specs=(rows, P("fsdp", None, None, None), *weights, rows),
        out_specs=(rows, rows, *weights),
        check_vma=False,
    )
```

time: 184 us -> 158 us (0.86)
  Pallas kernels: 182 us -> 157 us
    pallas_call x1, Pallas kernels: 179 us -> 154 us  [local(): pl.pallas_call(functools.partial(step_kernel, grad_scale, factor), out_sh...]
where the time goes in v3:
time: 158 us
  Pallas kernels  157 us (99%)
    pallas_call x1, Pallas kernels, local(): pl.pallas_call(functools.partial(step_kernel, grad_scale, factor), out_sh...  154 us

profile of v3, /device:TPU:1, one launch (start us, length us, event | category | flops | bytes accessed | tf_op | source)
XLA Modules:
  0.0 157.9 jit_solution(9778338983432837885)
XLA Ops:
  0.6 154.2 %shard_map.118 = (bf16[128,1536]{1,0:T(8,128)(2,1)}, f32[128,1536]{1,0:T(8,128)}, f32[3,48,384]{2,1,0:T(8,128)}, f32[48,384]{1,0:T(8,128)}, f32[48,1536]{1,0:T(8,128)}, /*index=5*/f32[48,1536]{1,0:T(8,128)}) custom-call(bf16[128,1536]{1,0:T(8,128)(2,1)} %bitcast.25, f32[6,1,1536]{2,1,0:T(1,128)} %bitcast.30, bf16[3,48,384]{2,1,0:T(8,128)(2,1)} %bitcast.29, ...), custom_call_target="tpu_custom_call" | custom-call | tf_op jit(solution)/shard_map/pallas_call | solution.py:937
  154.8 2.8 %shard_map.119 = (bf16[128,1536]{1,0:T(8,128)(2,1)}, f32[128,1536]{1,0:T(8,128)}, f32[3,48,384]{2,1,0:T(8,128)}, f32[48,384]{1,0:T(8,128)}, f32[48,1536]{1,0:T(8,128)}, /*index=5*/f32[48,1536]{1,0:T(8,128)}) custom-call(bf16[128,1536]{1,0:T(8,128)(2,1)} %get-tuple-element.18.refs_0_, f32[128,1536]{1,0:T(8,128)} %get-tuple-element.19.refs_1_, ...), custom_call_target="tpu_custom_call" | custom-call | tf_op jit(solution)/shard_map/pallas_call | solution.py:917

commit v4 on v3

--- a/solution.py
+++ b/solution.py
@@ -89,6 +89,18 @@
         self.open = []
 
 
+def launch(src, dst, ssem, rsem, dev):
+    pltpu.make_async_remote_copy(
+        src_ref=src, dst_ref=dst, send_sem=ssem, recv_sem=rsem, device_id=dev, device_id_type=MESH
+    ).start()
+
+
+def drained(ref, ssem, dev):
+    pltpu.make_async_remote_copy(
+        src_ref=ref, dst_ref=ref, send_sem=ssem, recv_sem=ssem, device_id=dev, device_id_type=MESH
+    ).wait_send()
+
+
 def arrive(ref, rsem, dev):
     pltpu.make_async_remote_copy(
         src_ref=ref, dst_ref=ref, send_sem=rsem, recv_sem=rsem, device_id=dev, device_id_type=MESH
@@ -112,7 +124,7 @@
 
     def go(self, level, to, p, q, which, i):
         ref = self.part(p, q, which)
-        self.sends.start(ref, ref, self.ssem.at[i], self.rsem.at[i], self.me.near(self.axes[level], to))
+        launch(ref, ref, self.ssem.at[level], self.rsem.at[i], self.me.near(self.axes[level], to))
 
     def got(self, p, q, which, i):
         arrive(self.part(p, q, which), self.rsem.at[i], self.me.near(self.axes[0], 1))
@@ -125,17 +137,15 @@
         self.got(-1, 0, "all", 0)
         self.go(0, 1, -1, 0, "lo", 2)
         self.got(1, 0, "all", 1)
-        self.go(0, -1, 1, 0, "hi", 3)
+        self.go(0, -1, 1, 0, "hi", 2)
 
     def last(self):
-        self.got(2, 0, "lo", 2)
-        self.got(2, 0, "hi", 3)
+        self.got(2, 0, "all", 2)
 
     def out(self, *ps):
         for p in ps:
-            i = 4 + (p + 1) * 2
-            self.go(1, 1, p, 0, "all", i)
-            self.go(1, -1, p, 0, "all", i + 1)
+            self.go(1, 1, p, 0, "all", 3)
+            self.go(1, -1, p, 0, "all", 4)
 
     def own(self):
         self.out(0)
@@ -147,16 +157,18 @@
         self.out(2)
 
     def relay(self):
-        for p in (0, -1, 1, 2):
-            self.got(p, -1, "all", 4 + (p + 1) * 2)
-        self.go(1, 1, None, -1, "lo", 12)
-        for p in (0, -1, 1, 2):
-            self.got(p, 1, "all", 5 + (p + 1) * 2)
-        self.go(1, -1, None, 1, "hi", 13)
+        self.got(None, -1, "all", 3)
+        self.go(1, 1, None, -1, "lo", 5)
+        self.got(None, 1, "all", 4)
+        self.go(1, -1, None, 1, "hi", 5)
 
     def close(self):
-        self.got(None, 2, "lo", 12)
-        self.got(None, 2, "hi", 13)
+        self.got(None, 2, "all", 5)
+
+    def drain(self):
+        cols = self.cols["all"]
+        drained(self.w.at[0, pl.ds(0, 3), 0, :, cols], self.ssem.at[0], self.me.near("z", 1))
+        drained(self.w.at[pl.ds(0, 3), pl.ds(0, 4), 0, :, cols], self.ssem.at[1], self.me.near("z", 1))
 
 
 def wider(ref_value):
@@ -191,9 +203,8 @@
         return self.inner[which].size, 0
 
     def send(self, level, step, which, dst, i, to):
-        i = level * 6 + i
-        self.sends.start(
-            self.g.at[self.spot(level, step, which)], dst, self.ssem.at[i], self.rsem.at[i],
+        launch(
+            self.g.at[self.spot(level, step, which)], dst, self.ssem.at[level], self.rsem.at[level * 2 + i],
             self.me.near(self.axes[level], to),
         )
 
@@ -205,31 +216,39 @@
 
     def far(self, level):
         for to, which, i in ((1, "lo", 0), (-1, "hi", 1)):
-            self.send(level, 2, which, self.way(level, i, which), i, to)
+            self.send(level, 2, which, self.way(level, i, which), 0, to)
 
     def rest(self, level):
         for to, which, i in ((1, "hi", 0), (-1, "lo", 1)):
-            self.send(level, to, which, self.near(level, i, which), 4 + i, to)
+            self.send(level, to, which, self.near(level, i, which), 1, to)
 
     def both(self, level):
         self.far(level)
         self.rest(level)
 
     def relay(self, level):
+        arrive(self.g.at[self.spot(level, 0, "all")], self.rsem.at[level * 2], self.me.near(self.axes[level], 1))
         for to, which, i in ((1, "lo", 0), (-1, "hi", 1)):
             buf = self.way(level, i, which)
-            arrive(buf, self.rsem.at[level * 6 + i], self.me.near(self.axes[level], -to))
             spot = self.spot(level, to, which)
             self.g[spot] = (wider(self.g[spot]) + wider(buf[...])).astype(BF16)
         for to, which, i in ((1, "lo", 0), (-1, "hi", 1)):
-            self.send(level, to, which, self.near(level, i, which), 2 + i, to)
+            self.send(level, to, which, self.near(level, i, which), 1, to)
 
     def total(self, level):
         near = self.bufs[level][1]
-        for which, i, j in (("hi", 0, 4), ("lo", 1, 5), ("lo", 0, 2), ("hi", 1, 3)):
-            arrive(self.near(level, i, which), self.rsem.at[level * 6 + j], self.me.near(self.axes[level], 1))
+        arrive(near, self.rsem.at[level * 2 + 1], self.me.near(self.axes[level], 1))
         spot = self.spot(level, 0, "all")
         return spot, wider(self.g[spot]) + wider(near[0]) + wider(near[1])
+
+    def drain_at(self, level):
+        places = pl.ds(0, 3) if level == 0 else 0
+        wide = pl.ds(0, 4) if level == 0 else pl.ds(0, 3)
+        drained(self.g.at[places, wide, 0, :, self.cols["all"]], self.ssem.at[level], self.me.near("z", 1))
+
+    def drain(self):
+        self.drain_at(0)
+        self.drain_at(1)
 
     def fold(self):
         spot, total = self.total(0)
@@ -238,20 +257,20 @@
 
 class FineScatter(Scatter):
     slots = {2: 0, 1: 1, -1: 2, 0: 3}
-    lines = (0, 12, 18, 24)
 
     def place(self, q, p, which):
         at = {self.axes[0]: self.me.ring(self.axes[0], q), self.axes[1]: self.me.ring(self.axes[1], p)}
         return (at["z"], at["y"], self.xb, slice(None), self.cols[which])
 
     def give(self, q, p, which, dst, i, to):
-        i = self.lines[self.slots[p]] + i
-        self.sends.start(
-            self.g.at[self.place(q, p, which)], dst, self.ssem.at[i], self.rsem.at[i], self.me.near(self.axes[0], to)
+        slot = self.slots[p]
+        launch(
+            self.g.at[self.place(q, p, which)], dst, self.ssem.at[2 + slot], self.rsem.at[4 + slot * 2 + i],
+            self.me.near(self.axes[0], to),
         )
 
-    def take(self, dst, p, i):
-        arrive(dst, self.rsem.at[self.lines[self.slots[p]] + i], self.me.near(self.axes[0], 1))
+    def take(self, ref, p, i):
+        arrive(ref, self.rsem.at[4 + self.slots[p] * 2 + i], self.me.near(self.axes[0], 1))
 
     def side(self, i, p, which):
         return self.bufs[0][1].at[i, self.slots[p], :, self.inner[which]]
@@ -262,31 +281,35 @@
     def far0(self, *ps):
         for p in ps:
             for to, which, i in ((1, "lo", 0), (-1, "hi", 1)):
-                self.give(2, p, which, self.step(i, p, which), i, to)
+                self.give(2, p, which, self.step(i, p, which), 0, to)
 
     def rest0(self, *ps):
         for p in ps:
             for to, which, i in ((1, "hi", 0), (-1, "lo", 1)):
-                self.give(to, p, which, self.side(i, p, which), 4 + i, to)
+                self.give(to, p, which, self.side(i, p, which), 1, to)
 
     def relay0(self, *ps):
         for p in ps:
+            self.take(self.g.at[self.place(0, p, "all")], p, 0)
             for to, which, i in ((1, "lo", 0), (-1, "hi", 1)):
-                buf = self.step(i, p, which)
-                self.take(buf, p, i)
                 spot = self.place(to, p, which)
-                self.g[spot] = pack(wider(self.g[spot]) + wider(buf[...]))
+                self.g[spot] = pack(wider(self.g[spot]) + wider(self.step(i, p, which)[...]))
             for to, which, i in ((1, "lo", 0), (-1, "hi", 1)):
-                self.give(to, p, which, self.side(i, p, which), 2 + i, to)
+                self.give(to, p, which, self.side(i, p, which), 1, to)
 
     def fold0(self, *ps):
         for p in ps:
-            for which, i, j in (("hi", 0, 4), ("lo", 1, 5), ("lo", 0, 2), ("hi", 1, 3)):
-                self.take(self.side(i, p, which), p, j)
+            near = self.bufs[0][1]
+            self.take(near.at[:, self.slots[p]], p, 1)
             spot = self.place(0, p, "all")
-            near = self.bufs[0][1]
             total = wider(self.g[spot]) + wider(near[0, self.slots[p]]) + wider(near[1, self.slots[p]])
             self.g[spot] = pack(total)
+
+    def drain(self):
+        self.drain_at(1)
+        for slot in range(4):
+            ref = self.g.at[0, pl.ds(0, 3), 0, :, self.cols["all"]]
+            drained(ref, self.ssem.at[2 + slot], self.me.near("z", 1))
 
 
 DMA = pltpu.SemaphoreType.DMA
@@ -797,39 +820,41 @@
     x_dm.start()
     ag("s0", "i0", "f1", "o1", "l0", "e0", "f2", "s1", "i1", "l1", "e1", "r0", "s2", "f3")
     x_a1.relay()
-    ag("o2", "i2", "l2", "r1", "e2", "o3", "s3", "i3")
+    ag("o2", "i2", "r1", "l2", "e2", "o3", "s3", "i3")
     x_dm.relay()
-    ag("l3", "e3", "c0")
+    ag("c0")
     x_a1.near()
     x_a1.far()
     ag("c1")
     forward(a1, mine, wa, 0, 3 * QKV, put(packed, mine))
+    ag("l3", "e3")
     forward(a1, other, wa, 0, 3 * QKV, put(packed, other))
-    ag("s4", "r2")
+    ag("r2", "s4", "i4")
     heads(attend, 0, 1)
-    ag("r3", "i4", "f5")
+    ag("r3", "l4", "e4", "f5", "o5")
     heads(attend, 1, 3)
     ag("c2", "c3")
     share(y_att, att, 3 * QKV, QKV)
     x_dm.spread()
-    ag("l4", "e4", "s5", "o5", "i5", "l5", "e5")
+    ag("s5", "i5", "l5", "e5")
     x_dm.last()
+    ag("r4")
+    norm_and_send(0)
+    ag("r5")
+    norm_and_send(1)
+    x_a2s[0].relay()
+    y_att.sends.close()
     x_dm.own()
     x_dm.sides()
     x_dm.far()
-    ag("r4")
-    norm_and_send(0)
-    norm_and_send(1)
-    ag("r5")
-    x_a2s[0].relay()
-    y_att.sends.close()
     all_of(x_a2s, "own")
     ag("c4", "c5")
     pl.loop(0, 2)(backs)
     x_a2s[1].relay()
     hidden(me.x)
+    all_of(x_a2s, "spread")
     pl.loop(2, 4)(backs)
-    all_of(x_a2s, "spread", "sides")
+    all_of(x_a2s, "sides")
     pl.loop(0, 2)(sides)
     all_of(x_a2s, "last")
 
@@ -884,8 +909,8 @@
     rsc("F8", "F9", "N8", "N9", "s2", "s3", "R6a", "R7a", "R6b", "R7b", "R6c", "R7c", "e0")
     y_ffn.relay()
     share(y_first, packed, 0, 3 * QKV)
-    rsc("R8a", "R9a", "R8b", "R9b", "R8c", "R9c", "e2", "D4", "G4", "H4", "D5", "G5", "H5")
-    rsc("D6a", "G6", "D7a", "G7", "D6b", "H6", "D7b", "H7", "D6c", "D7c")
+    rsc("R8a", "R9a", "R8b", "R9b", "R8c", "R9c", "D4", "G4", "H4", "D5", "G5", "H5")
+    rsc("D6a", "G6", "D7a", "G7", "D6b", "H6", "D7b", "H7", "D6c", "D7c", "e2")
     rsc("D8a", "G8", "D9a", "G9", "D8b", "H8", "D9b", "H9", "D8c", "D9c", "s4", "s5", "s6", "s7", "s8", "s9")
     rsc("e4", "e6", "e8")
     y_ffn.wait()
@@ -898,6 +923,11 @@
         arrive(xf.at[group], yr.at[group], me.across())
         out[:, pl.ds(other_f, HALF)] = wider(xf[group])
     rsc("e5", "e7", "e9")
+    for piece in pieces:
+        for half in piece:
+            half.drain()
+    for scatter in scatters:
+        scatter.drain()
     sends.close()
     y_first.sends.close()
     y_ffn.sends.close()
@@ -952,7 +982,7 @@
             vm(8, OWN, HALF), vm(8, OWN, HALF, dtype=F32), vm(8, OWN, HALF),
             vm(*ring), vm(2, OWN, WIDTH), vm(OWN, WIDTH), vm(OWN, WIDTH),
             vm(2, 4, OWN, WIDTH), vm(2, 2, OWN, HALF), vm(2, 2, OWN, WIDTH), vm(OWN, WIDTH, dtype=F32),
-            DMA((10, 14)), DMA((10, 14)), DMA((10, 30)), DMA((10, 30)),
+            DMA((10, 2)), DMA((10, 6)), DMA((10, 6)), DMA((10, 12)),
             DMA((4,)), DMA((4,)), DMA((5,)), DMA((5,)), DMA((11, 11)), DMA((11, 11)), DMA((12,)),
         ],
         compiler_params=pltpu.CompilerParams(

time: 158 us -> 150 us (0.949)
  Pallas kernels: 157 us -> 149 us
    pallas_call x1, Pallas kernels: 154 us -> 146 us  [local(): pl.pallas_call(functools.partial(step_kernel, grad_scale, factor), out_sh...]
where the time goes in v4:
time: 150 us; the launch traced here: 149 us
  Pallas kernels  149 us (99%)
    pallas_call x1, Pallas kernels, local(): pl.pallas_call(functools.partial(step_kernel, grad_scale, factor), out_sh...  146 us

profile of v4, /device:TPU:1, one launch (start us, length us, event | category | flops | bytes accessed | tf_op | source)
XLA Modules:
  0.0 149.4 jit_solution(16963014434838303764)
XLA Ops:
  0.6 145.8 %shard_map.118 = (bf16[128,1536]{1,0:T(8,128)(2,1)}, f32[128,1536]{1,0:T(8,128)}, f32[3,48,384]{2,1,0:T(8,128)}, f32[48,384]{1,0:T(8,128)}, f32[48,1536]{1,0:T(8,128)}, /*index=5*/f32[48,1536]{1,0:T(8,128)}) custom-call(bf16[128,1536]{1,0:T(8,128)(2,1)} %bitcast.25, f32[6,1,1536]{2,1,0:T(1,128)} %bitcast.30, bf16[3,48,384]{2,1,0:T(8,128)(2,1)} %bitcast.29, ...), custom_call_target="tpu_custom_call" | custom-call | tf_op jit(solution)/shard_map/pallas_call | solution.py:967
  146.4 2.8 %shard_map.119 = (bf16[128,1536]{1,0:T(8,128)(2,1)}, f32[128,1536]{1,0:T(8,128)}, f32[3,48,384]{2,1,0:T(8,128)}, f32[48,384]{1,0:T(8,128)}, f32[48,1536]{1,0:T(8,128)}, /*index=5*/f32[48,1536]{1,0:T(8,128)}) custom-call(bf16[128,1536]{1,0:T(8,128)(2,1)} %get-tuple-element.18.refs_0_, f32[128,1536]{1,0:T(8,128)} %get-tuple-element.19.refs_1_, ...), custom_call_target="tpu_custom_call" | custom-call | tf_op jit(solution)/shard_map/pallas_call | solution.py:947

commit v5 on v4

--- a/solution.py
+++ b/solution.py
@@ -332,7 +332,10 @@
 
     def push(self, block, i, dev):
         ref = self.buf.at[block, self.rows]
-        self.sends.start(ref, ref, self.ssem.at[i], self.rsem.at[i], dev)
+        launch(ref, ref, self.ssem.at[0], self.rsem.at[i], dev)
+
+    def drain(self):
+        drained(self.buf.at[pl.ds(0, 3), self.rows], self.ssem.at[0], self.me.core())
 
     def start(self):
         self.push(self.me.s, 0, self.me.chip())
@@ -353,13 +356,14 @@
 class SeqScatter:
     def __init__(self, me, part, swap, mine, theirs, ssem, rsem):
         self.me, self.part, self.swap, self.mine, self.theirs = me, part, swap, mine, theirs
-        self.ssem, self.rsem, self.sends = ssem, rsem, Sends()
+        self.ssem, self.rsem = ssem, rsem
+
+    def drain(self):
+        drained(self.part.at[pl.ds(0, 3)], self.ssem.at[0], self.me.core())
 
     def give(self, i):
         xl = self.me.xl if i else 1 - self.me.xl
-        self.sends.start(
-            self.part.at[xl * 2 + 1 - self.me.c], self.swap.at[i], self.ssem.at[i], self.rsem.at[i], self.me.core()
-        )
+        launch(self.part.at[xl * 2 + 1 - self.me.c], self.swap.at[i], self.ssem.at[0], self.rsem.at[i], self.me.core())
 
     def cross(self):
         arrive(self.swap.at[0], self.rsem.at[0], self.me.core())
@@ -370,9 +374,7 @@
         for i, rows in enumerate(CHUNKS):
             by_rows(merge, rows)
             r = pl.ds(*rows)
-            self.sends.start(
-                self.mine.at[r], self.theirs.at[r], self.ssem.at[2 + i], self.rsem.at[2 + i], self.me.chip()
-            )
+            launch(self.mine.at[r], self.theirs.at[r], self.ssem.at[0], self.rsem.at[2 + i], self.me.chip())
 
     def wait(self, i):
         if i == 0:
@@ -394,38 +396,38 @@
         return self.buf.at[self.me.chip_at(step) * 2 + (self.me.c if mine else 1 - self.me.c), self.rows, cols]
 
     def push(self, ref, i, dev):
-        self.sends.start(ref, ref, self.ssem.at[i], self.rsem.at[i], dev)
+        launch(ref, ref, self.ssem.at[0], self.rsem.at[i], dev)
+
+    def drain(self):
+        drained(self.buf.at[pl.ds(0, 7), self.rows], self.ssem.at[0], self.me.core())
 
     def start(self):
-        for cols, step, i in ((LEFT, 1, 0), (RIGHT, -1, 1), (RIGHT, 1, 9), (LEFT, -1, 10)):
+        for cols, step, i in ((LEFT, 1, 0), (RIGHT, -1, 1), (RIGHT, 1, 2), (LEFT, -1, 2)):
             self.push(self.at(0, cols=cols), i, self.me.along(step))
-        self.push(self.at(0), 2, self.me.core())
+        self.push(self.at(0), 3, self.me.core())
 
     def relay(self):
         for step, cols, i in ((-1, LEFT, 0), (1, RIGHT, 1)):
             arrive(self.at(step, cols=cols), self.rsem.at[i], self.me.core())
-            self.push(self.at(step, cols=cols), 3 + i, self.me.along(-step))
+            self.push(self.at(step, cols=cols), 4, self.me.along(-step))
 
     def spread(self):
-        for step, cols, i in ((-1, RIGHT, 0), (1, LEFT, 1)):
-            arrive(self.at(step, cols=cols), self.rsem.at[9 + i], self.me.core())
-            self.push(self.at(step), 5 + i, self.me.core())
+        arrive(self.at(1), self.rsem.at[2], self.me.core())
+        for step in (-1, 1):
+            self.push(self.at(step), 5, self.me.core())
 
     def last(self):
-        for cols, i in ((LEFT, 0), (RIGHT, 1)):
-            arrive(self.at(2, cols=cols), self.rsem.at[3 + i], self.me.core())
-            self.push(self.at(2, cols=cols), 7 + i, self.me.core())
+        arrive(self.at(2), self.rsem.at[4], self.me.core())
+        self.push(self.at(2), 6, self.me.core())
 
     def own(self):
-        arrive(self.at(0, False), self.rsem.at[2], self.me.core())
+        arrive(self.at(0, False), self.rsem.at[3], self.me.core())
 
     def sides(self):
-        for step, i in ((-1, 5), (1, 6)):
-            arrive(self.at(step, False), self.rsem.at[i], self.me.core())
+        arrive(self.buf.at[pl.ds(0, 2), self.rows], self.rsem.at[5], self.me.core())
 
     def far(self):
-        for cols, i in ((LEFT, 7), (RIGHT, 8)):
-            arrive(self.at(2, False, cols), self.rsem.at[i], self.me.core())
+        arrive(self.at(2, False), self.rsem.at[6], self.me.core())
 
 
 class RingScatter:
@@ -433,7 +435,7 @@
 
     def __init__(self, me, part, swap, away, near, rows, ssem, rsem):
         self.me, self.part, self.swap, self.away, self.near = me, part, swap, away, near
-        self.span, self.ssem, self.rsem, self.sends = rows, ssem, rsem, Sends()
+        self.span, self.ssem, self.rsem = rows, ssem, rsem
         self.r = pl.ds(*rows)
 
     def block(self, step):
@@ -441,16 +443,19 @@
 
     def give(self, j):
         src = self.part.at[self.me.chip_at(self.order[j]) * 2 + 1 - self.me.c]
-        self.sends.start(src, self.swap.at[j], self.ssem.at[j], self.rsem.at[j], self.me.core())
+        launch(src, self.swap.at[j], self.ssem.at[0], self.rsem.at[j], self.me.core())
+
+    def drain(self):
+        if self.span[0] == 0:
+            drained(self.part.at[pl.ds(0, 4)], self.ssem.at[0], self.me.core())
+        drained(self.part.at[pl.ds(0, 3), self.r], self.ssem.at[1], self.me.core())
 
     def swapped(self, j):
         if self.span[0] == 0:
             arrive(self.swap.at[j], self.rsem.at[j], self.me.core())
 
     def push(self, step, cols, dst, i, to):
-        self.sends.start(
-            self.part.at[self.block(step), self.r, cols], dst, self.ssem.at[i], self.rsem.at[i], self.me.along(to)
-        )
+        launch(self.part.at[self.block(step), self.r, cols], dst, self.ssem.at[1], self.rsem.at[i], self.me.along(to))
 
     def out(self):
         self.swapped(0)
@@ -461,7 +466,7 @@
 
         by_rows(merge, self.span)
         self.push(2, LEFT, self.away.at[0, self.r], 4, 1)
-        self.push(2, RIGHT, self.away.at[1, self.r], 5, -1)
+        self.push(2, RIGHT, self.away.at[1, self.r], 4, -1)
 
     def rest(self):
         for step, j, i, cols in ((1, 1, 0, RIGHT), (-1, 2, 1, LEFT)):
@@ -472,11 +477,11 @@
                 self.part[block, r, cols] = pack(wider(self.part[block, r, cols]) + wider(self.swap[j, r, cols]))
 
             by_rows(merge, self.span)
-            self.push(step, cols, self.near.at[i, self.r, cols], 8 + i, step)
+            self.push(step, cols, self.near.at[i, self.r, cols], 5, step)
 
     def relay(self):
+        arrive(self.away.at[:, self.r], self.rsem.at[4], self.me.core())
         for step, j, i, cols in ((1, 1, 0, LEFT), (-1, 2, 1, RIGHT)):
-            arrive(self.away.at[i, self.r], self.rsem.at[4 + i], self.me.core())
             block = self.block(step)
 
             def merge(r):
@@ -484,13 +489,11 @@
                 self.part[block, r, cols] = pack(both + wider(self.away[i, r]))
 
             by_rows(merge, self.span)
-            self.push(step, cols, self.near.at[i, self.r, cols], 6 + i, step)
+            self.push(step, cols, self.near.at[i, self.r, cols], 5, step)
 
     def wait(self):
         self.swapped(3)
-        for i, cols, rest in ((0, LEFT, RIGHT), (1, RIGHT, LEFT)):
-            arrive(self.near.at[i, self.r, rest], self.rsem.at[8 + i], self.me.core())
-            arrive(self.near.at[i, self.r, cols], self.rsem.at[6 + i], self.me.core())
+        arrive(self.near.at[:, self.r], self.rsem.at[5], self.me.core())
 
     def rows(self, r):
         own = wider(self.part[self.block(0), r]) + wider(self.swap[3, r])
@@ -843,7 +846,7 @@
     ag("r5")
     norm_and_send(1)
     x_a2s[0].relay()
-    y_att.sends.close()
+    y_att.drain()
     x_dm.own()
     x_dm.sides()
     x_dm.far()
@@ -877,9 +880,8 @@
     rsc("r0", "r1", "f2", "f3")
     back_and_send(0)
     back_and_send(1)
-    y_backs[0].sends.close()
-    y_backs[1].sends.close()
-    a2_sends.close()
+    all_of(y_backs, "drain")
+    all_of(x_a2s, "drain")
     backward(act, me.chip_at(2), wf, HALF, HALF, pf)
     y_ffn.give(0)
     backward(act, me.chip_at(1), wf, HALF, HALF, pf)
@@ -928,9 +930,8 @@
             half.drain()
     for scatter in scatters:
         scatter.drain()
+    all_of([x_a1, x_dm, y_first, y_ffn] + x_das, "drain")
     sends.close()
-    y_first.sends.close()
-    y_ffn.sends.close()
 
 
 def copy_kernel(*refs):
@@ -983,7 +984,7 @@
             vm(*ring), vm(2, OWN, WIDTH), vm(OWN, WIDTH), vm(OWN, WIDTH),
             vm(2, 4, OWN, WIDTH), vm(2, 2, OWN, HALF), vm(2, 2, OWN, WIDTH), vm(OWN, WIDTH, dtype=F32),
             DMA((10, 2)), DMA((10, 6)), DMA((10, 6)), DMA((10, 12)),
-            DMA((4,)), DMA((4,)), DMA((5,)), DMA((5,)), DMA((11, 11)), DMA((11, 11)), DMA((12,)),
+            DMA((4,)), DMA((4,)), DMA((5,)), DMA((5,)), DMA((11, 2)), DMA((11, 7)), DMA((12,)),
         ],
         compiler_params=pltpu.CompilerParams(
             collective_id=0, has_side_effects=True, vmem_limit_bytes=67043328

time: 150 us -> 148 us (0.987)
  Pallas kernels: 149 us -> 147 us
    pallas_call x1, Pallas kernels: 146 us -> 144 us  [local(): pl.pallas_call(functools.partial(step_kernel, grad_scale, factor), out_sh...]
where the time goes in v5:
time: 148 us
  Pallas kernels  147 us (99%)
    pallas_call x1, Pallas kernels, local(): pl.pallas_call(functools.partial(step_kernel, grad_scale, factor), out_sh...  144 us

profile of v5, /device:TPU:1, one launch (start us, length us, event | category | flops | bytes accessed | tf_op | source)
XLA Modules:
  0.0 147.9 jit_solution(16878151787008860406)
XLA Ops:
  0.6 144.2 %shard_map.118 = (bf16[128,1536]{1,0:T(8,128)(2,1)}, f32[128,1536]{1,0:T(8,128)}, f32[3,48,384]{2,1,0:T(8,128)}, f32[48,384]{1,0:T(8,128)}, f32[48,1536]{1,0:T(8,128)}, /*index=5*/f32[48,1536]{1,0:T(8,128)}) custom-call(bf16[128,1536]{1,0:T(8,128)(2,1)} %bitcast.25, f32[6,1,1536]{2,1,0:T(1,128)} %bitcast.30, bf16[3,48,384]{2,1,0:T(8,128)(2,1)} %bitcast.29, ...), custom_call_target="tpu_custom_call" | custom-call | tf_op jit(solution)/shard_map/pallas_call | solution.py:968
  144.9 2.8 %shard_map.119 = (bf16[128,1536]{1,0:T(8,128)(2,1)}, f32[128,1536]{1,0:T(8,128)}, f32[3,48,384]{2,1,0:T(8,128)}, f32[48,384]{1,0:T(8,128)}, f32[48,1536]{1,0:T(8,128)}, /*index=5*/f32[48,1536]{1,0:T(8,128)}) custom-call(bf16[128,1536]{1,0:T(8,128)(2,1)} %get-tuple-element.18.refs_0_, f32[128,1536]{1,0:T(8,128)} %get-tuple-element.19.refs_1_, ...), custom_call_target="tpu_custom_call" | custom-call | tf_op jit(solution)/shard_map/pallas_call | solution.py:948

commit v6 on v5

--- a/solution.py
+++ b/solution.py
@@ -908,7 +908,7 @@
     rsc("F6", "F7", "N6", "N7", "R4", "R5")
     heads(attend_back, 2, 3)
     gradient(a1, packed.at[:, :, pl.ds(HALF, QKV)], ga, HALF, QKV)
-    rsc("F8", "F9", "N8", "N9", "s2", "s3", "R6a", "R7a", "R6b", "R7b", "R6c", "R7c", "e0")
+    rsc("F8", "F9", "s2", "s3", "R6a", "R7a", "R6b", "R7b", "R6c", "R7c", "N8", "N9", "e0")
     y_ffn.relay()
     share(y_first, packed, 0, 3 * QKV)
     rsc("R8a", "R9a", "R8b", "R9b", "R8c", "R9c", "D4", "G4", "H4", "D5", "G5", "H5")

time: 148 us -> 148 us (level)
  no operation moved by 1% of the time
where the time goes in v6:
time: 148 us
  Pallas kernels  147 us (99%)
    pallas_call x1, Pallas kernels, local(): pl.pallas_call(functools.partial(step_kernel, grad_scale, factor), out_sh...  144 us

profile of v6, /device:TPU:1, one launch (start us, length us, event | category | flops | bytes accessed | tf_op | source)
XLA Modules:
  0.0 147.9 jit_solution(16725832615172143327)
XLA Ops:
  0.6 144.2 %shard_map.118 = (bf16[128,1536]{1,0:T(8,128)(2,1)}, f32[128,1536]{1,0:T(8,128)}, f32[3,48,384]{2,1,0:T(8,128)}, f32[48,384]{1,0:T(8,128)}, f32[48,1536]{1,0:T(8,128)}, /*index=5*/f32[48,1536]{1,0:T(8,128)}) custom-call(bf16[128,1536]{1,0:T(8,128)(2,1)} %bitcast.25, f32[6,1,1536]{2,1,0:T(1,128)} %bitcast.30, bf16[3,48,384]{2,1,0:T(8,128)(2,1)} %bitcast.29, ...), custom_call_target="tpu_custom_call" | custom-call | tf_op jit(solution)/shard_map/pallas_call | solution.py:968
  144.9 2.8 %shard_map.119 = (bf16[128,1536]{1,0:T(8,128)(2,1)}, f32[128,1536]{1,0:T(8,128)}, f32[3,48,384]{2,1,0:T(8,128)}, f32[48,384]{1,0:T(8,128)}, f32[48,1536]{1,0:T(8,128)}, /*index=5*/f32[48,1536]{1,0:T(8,128)}) custom-call(bf16[128,1536]{1,0:T(8,128)(2,1)} %get-tuple-element.18.refs_0_, f32[128,1536]{1,0:T(8,128)} %get-tuple-element.19.refs_1_, ...), custom_call_target="tpu_custom_call" | custom-call | tf_op jit(solution)/shard_map/pallas_call | solution.py:948

commit v7 on v6

--- a/solution.py
+++ b/solution.py
@@ -550,12 +550,12 @@
         (wi.at[:, pl.ds(mine_f, HALF)], home_f.at[:, LEFT]),
         (wb.at[:, pl.ds(mine_f, HALF)], home_f.at[:, RIGHT]),
     ]
-    loads = [pltpu.make_async_copy(src, dst, csem.at[i]) for i, (src, dst) in enumerate(parts)]
+    loads = [pltpu.make_async_copy(src, dst, csem.at[i // 10]) for i, (src, dst) in enumerate(parts)]
     for load in loads:
         load.start()
     greet(torus_peers(me))
-    for load in loads:
-        load.wait()
+    for i, home in enumerate((home_a, home_f)):
+        pltpu.make_async_copy(home, home, csem.at[i]).wait()
     mine, other = me.xl, 1 - me.xl
 
     def m(i):
@@ -984,7 +984,7 @@
             vm(*ring), vm(2, OWN, WIDTH), vm(OWN, WIDTH), vm(OWN, WIDTH),
             vm(2, 4, OWN, WIDTH), vm(2, 2, OWN, HALF), vm(2, 2, OWN, WIDTH), vm(OWN, WIDTH, dtype=F32),
             DMA((10, 2)), DMA((10, 6)), DMA((10, 6)), DMA((10, 12)),
-            DMA((4,)), DMA((4,)), DMA((5,)), DMA((5,)), DMA((11, 2)), DMA((11, 7)), DMA((12,)),
+            DMA((4,)), DMA((4,)), DMA((5,)), DMA((5,)), DMA((11, 2)), DMA((11, 7)), DMA((2,)),
         ],
         compiler_params=pltpu.CompilerParams(
             collective_id=0, has_side_effects=True, vmem_limit_bytes=67043328

time: 148 us -> 148 us (level)
  no operation moved by 1% of the time
where the time goes in v7:
time: 148 us
  Pallas kernels  147 us (99%)
    pallas_call x1, Pallas kernels, local(): pl.pallas_call(functools.partial(step_kernel, grad_scale, factor), out_sh...  144 us

profile of v7, /device:TPU:1, one launch (start us, length us, event | category | flops | bytes accessed | tf_op | source)
XLA Modules:
  0.0 147.8 jit_solution(10225730245104798669)
XLA Ops:
  0.6 144.1 %shard_map.118 = (bf16[128,1536]{1,0:T(8,128)(2,1)}, f32[128,1536]{1,0:T(8,128)}, f32[3,48,384]{2,1,0:T(8,128)}, f32[48,384]{1,0:T(8,128)}, f32[48,1536]{1,0:T(8,128)}, /*index=5*/f32[48,1536]{1,0:T(8,128)}) custom-call(bf16[128,1536]{1,0:T(8,128)(2,1)} %bitcast.25, f32[6,1,1536]{2,1,0:T(1,128)} %bitcast.30, bf16[3,48,384]{2,1,0:T(8,128)(2,1)} %bitcast.29, ...), custom_call_target="tpu_custom_call" | custom-call | tf_op jit(solution)/shard_map/pallas_call | solution.py:968
  144.8 2.8 %shard_map.119 = (bf16[128,1536]{1,0:T(8,128)(2,1)}, f32[128,1536]{1,0:T(8,128)}, f32[3,48,384]{2,1,0:T(8,128)}, f32[48,384]{1,0:T(8,128)}, f32[48,1536]{1,0:T(8,128)}, /*index=5*/f32[48,1536]{1,0:T(8,128)}) custom-call(bf16[128,1536]{1,0:T(8,128)(2,1)} %get-tuple-element.18.refs_0_, f32[128,1536]{1,0:T(8,128)} %get-tuple-element.19.refs_1_, ...), custom_call_target="tpu_custom_call" | custom-call | tf_op jit(solution)/shard_map/pallas_call | solution.py:948
